TPU v7x, 32 devices: a whole 2x2x4 slice. The times are simulated.
32 devices in a mesh: tm: 4 (over y, x), lat: 4 (over z), ens: 2 (over core).
Axes of the slice: x: 2, y: 2, z: 4, core: 2. Of those that a mesh axis runs over, the one named last changes fastest.
Arguments:
- increment: float32 [4, 4, 64, 1440], P('tm', None, 'lat'), may hold values from -6 to 6
- wind_lon: float32 [4, 4, 64, 1440], P('tm', None, 'lat'), may hold values from -0.45 to 0.45
- wind_lat: float32 [4, 4, 64, 1440], P('tm', None, 'lat'), may hold values from -0.45 to 0.45
- model_precision: float32 [4], replicated, may hold values from 0.5 to 4
- perturbations: float32 [32, 4, 64, 1440], P('ens', 'tm', 'lat'), may hold values from -0.24350093 to 0.24350093
- obs_rows: int32 [4, 128], P('tm', 'lat'), may hold values from 0 to 63
- obs_jacobian: float32 [4, 128, 16, 1440], P('tm', 'lat'), may hold values from -0.15625 to 0.15625
- obs_values: float32 [4, 128, 16], P('tm', 'lat'), may hold values from -6 to 6
- obs_precision: float32 [4, 128, 16], P('tm', 'lat'), may hold values from 0.5 to 2
- obs_counts: int32 [4, 128], P('tm', 'lat'), may hold values from 1 to 16
Outputs:
- grad_state: float32 [4, 4, 64, 1440], P('tm', None, 'lat')
- forcing_step: float32 [4, 64, 1440], P('tm', 'lat')
Inputs may be any that keep to these rules, and one draw needn't show every extreme that they name: `obs_rows`: block j of band b reads level r // 16 and latitude b * 16 + r % 16, where r is its entry; several blocks may read the same row. `obs_counts`: only the first count slots of a block hold observations.
All inputs are finite; a program needn't handle non-finite values.
Results may differ from a plain program's by a relative error of at most 0.0003.
Values sent between devices are 32-bit elements; how exact they have to be, the bound alone decides.
A program may use at most 64 MiB of HBM per device.

v0:
```python
import functools

import jax
import jax.numpy as jnp
from jax import lax
from jax.experimental import pallas as pl
from jax.experimental.pallas import tpu as pltpu
from jax.sharding import PartitionSpec as P

STEPS = 4
MESH = pl.DeviceIdType.MESH
HIGHEST = lax.Precision.HIGHEST
NT = (((1,), (1,)), ((), ()))
NN = (((1,), (0,)), ((), ()))


def mm(a, b, dims, precision=None):
    return lax.dot_general(a, b, dims, precision=precision, preferred_element_type=jnp.float32)


def split(value):
    hi = value.astype(jnp.bfloat16)
    lo = (value - hi.astype(jnp.float32)).astype(jnp.bfloat16)
    return hi, lo


def turn(value, steps, axis):
    return pltpu.roll(value, steps % value.shape[axis], axis)


def extend(ref, where, lon):
    width = ref.shape[-1]
    rem = lon % 128
    last = ref[where + (slice(0, 16), slice(width - 128, width))]
    before = ref[where + (slice(0, 16), slice(width - 256, width - 128))]
    first = ref[where + (slice(0, 16), slice(0, 128))]
    lane = lax.broadcasted_iota(jnp.int32, last.shape, 1)
    wrapped = jnp.where(lane < 128 - rem, turn(before, 128 - rem, 1), turn(last, 128 - rem, 1))
    right = jnp.where(lane < rem + (128 - rem) // 2, turn(first, rem, 1), wrapped)
    ref[where + (slice(0, 16), slice(width - 128, width))] = jnp.where(lane < rem, last, right)


def kernel(
    T, L, E,
    rows_hbm, cnt_hbm, val_hbm, prc_hbm, mp_hbm, inc_hbm, wlon_hbm, wlat_hbm, jac_hbm, pert_hbm,
    grad_v, pert_v, cb_v,
    rows_ref, cnt_ref, val_ref, prc_ref, mp_ref, inc_v, wlon_v, wlat_v, jac_v, jhi, jlo, wide, coef, adj,
    h_first, h_last, h_after, h_before, a_up_v, a_down_v, a_after, a_before,
    end_v, nxt_v, prior_v, forc, edge, rs_v, edge_v, ca_send, ca_v, cb_send,
    load_sem, h_ssem, h_rsem, a_ssem, a_rsem, t_ssem, t_rsem, e_ssem, e_rsem, p_ssem, p_rsem,
    rs_ssem, rs_rsem, ed_ssem, ed_rsem, ca_ssem, ca_rsem, cb_ssem, cb_rsem, g_ssem, g_rsem, all_sem,
):
    k, b, e = lax.axis_index("tm"), lax.axis_index("lat"), lax.axis_index("ens")
    half, crow, lon = inc_v.shape
    width = wide.shape[-1]
    members = pert_v.shape[1]
    slots, blocks = val_ref.shape
    flat = blocks * slots
    other = 1 - e
    own = pl.ds(e * half, half)

    loads = [
        pltpu.make_async_copy(inc_hbm.at[own], inc_v, load_sem.at[0]),
        pltpu.make_async_copy(wlon_hbm.at[own], wlon_v, load_sem.at[1]),
        pltpu.make_async_copy(wlat_hbm.at[own], wlat_v, load_sem.at[2]),
        pltpu.make_async_copy(jac_hbm, jac_v, load_sem.at[3]),
        pltpu.make_async_copy(pert_hbm, pert_v.at[e], load_sem.at[4]),
        pltpu.make_async_copy(rows_hbm, rows_ref, load_sem.at[5]),
        pltpu.make_async_copy(cnt_hbm, cnt_ref, load_sem.at[6]),
        pltpu.make_async_copy(val_hbm, val_ref, load_sem.at[7]),
        pltpu.make_async_copy(prc_hbm, prc_ref, load_sem.at[8]),
        pltpu.make_async_copy(mp_hbm, mp_ref, load_sem.at[9]),
    ]
    for item in loads[:3]:
        item.start()

    barrier = pltpu.get_barrier_semaphore()
    direct = T * L * E <= 64
    group = [(dt, de) for dt in range(T) for de in range(E) if dt or de]

    def mate(dt, de):
        return {"tm": lax.rem(k + dt, T), "ens": lax.rem(e + de, E)}

    for dt, de in group:
        pl.semaphore_signal(barrier, inc=1, device_id=mate(dt, de), device_id_type=MESH)
    for db in range(1, L):
        pl.semaphore_signal(barrier, inc=1, device_id={"lat": lax.rem(b + db, L)}, device_id_type=MESH)

    def remote(src, dst, ssem, rsem, device):
        return pltpu.make_async_remote_copy(
            src_ref=src, dst_ref=dst, send_sem=ssem, recv_sem=rsem, device_id=device, device_id_type=MESH
        )

    up = {"lat": lax.rem(b + 1, L)}
    down = {"lat": lax.rem(b + L - 1, L)}
    later_dev = {"tm": lax.rem(k + 1, T)}
    prior_dev = {"tm": lax.rem(k + T - 1, T)}
    partner = {"ens": other}
    has_up, has_down = b < L - 1, b > 0
    has_later, has_prior = k < T - 1, k > 0

    for item in loads[:3]:
        item.wait()
    for item in loads[4:5] + loads[3:4] + loads[5:]:
        item.start()
    for at, ref in enumerate((inc_v, wlon_v, wlat_v)):
        for i in range(half):
            wide[at, i, 0:16, 0:lon] = ref[i]
            extend(wide, (at, i), lon)
            h_first[i, at] = wide[at, i, 0:4]
            h_last[i, at] = wide[at, i, crow - 4 : crow]

    pl.semaphore_wait(barrier, len(group) + L - 1)
    if direct:
        for db in range(1, L):
            pl.semaphore_signal(all_sem, inc=1, device_id={"lat": lax.rem(b + db, L)}, device_id_type=MESH)

    h_up = [remote(h_last.at[i], h_before.at[i], h_ssem.at[0, i], h_rsem.at[0, i], up) for i in range(half)]
    h_down = [remote(h_first.at[i], h_after.at[i], h_ssem.at[1, i], h_rsem.at[1, i], down) for i in range(half)]
    e_copy = [remote(end_v.at[i], prior_v.at[i], e_ssem.at[i], e_rsem.at[i], later_dev) for i in range(half)]
    n_copy = remote(inc_v, nxt_v, t_ssem.at[0], t_rsem.at[0], prior_dev)

    for i in range(half):
        @pl.when(has_up)
        def _():
            h_up[i].start()

        @pl.when(has_down)
        def _():
            h_down[i].start()

    @pl.when(has_prior)
    def _():
        n_copy.start()

    loads[4].wait()
    p_copy = remote(pert_v.at[e], pert_v.at[e], p_ssem, p_rsem, partner)
    p_copy.start()

    @pl.when(jnp.logical_not(has_up))
    def _():
        h_after[...] = jnp.zeros_like(h_after)
        a_after[...] = jnp.zeros_like(a_after)

    @pl.when(jnp.logical_not(has_down))
    def _():
        h_before[...] = jnp.zeros_like(h_before)
        a_before[...] = jnp.zeros_like(a_before)

    @pl.when(jnp.logical_not(has_prior))
    def _():
        prior_v[...] = jnp.zeros_like(prior_v)

    edge_in = ((e == 0) & has_down) | ((e == E - 1) & has_up)

    @pl.when(jnp.logical_not(edge_in))
    def _():
        edge_v[...] = jnp.zeros_like(edge_v)

    for item in loads[5:]:
        item.wait()
    loads[3].wait()
    jhi[:, width - 128 : width] = jnp.zeros((flat, 128), jnp.bfloat16)
    jlo[:, width - 128 : width] = jnp.zeros((flat, 128), jnp.bfloat16)

    def cut(at, carry):
        some = pl.ds(pl.multiple_of(at * 32, 32), 32)
        hi, lo = split(jac_v[some, :])
        jhi[some, 0:lon] = hi
        jlo[some, 0:lon] = lo
        return carry

    lax.fori_loop(0, flat // 32, cut, 0)

    column = lax.broadcasted_iota(jnp.int32, (blocks, flat), 1)
    block = lax.broadcasted_iota(jnp.int32, (blocks, flat), 0)
    mine = (column >= block * slots) & (column < (block + 1) * slots)
    spread = mine.astype(jnp.float32)
    first_column = lax.broadcasted_iota(jnp.int32, (1, flat), 1)
    slot = (first_column % slots).astype(jnp.float32)
    tile_slot = lax.broadcasted_iota(jnp.int32, (slots, flat), 0)
    tile_column = lax.broadcasted_iota(jnp.int32, (slots, flat), 1) % slots
    tiled = (tile_slot == tile_column).astype(jnp.float32)

    def flatten(ref):
        return jnp.sum(mm(ref[...], spread, NN, HIGHEST) * tiled, axis=0, keepdims=True)

    values, precisions = flatten(val_ref), flatten(prc_ref)
    counts = mm(jnp.broadcast_to(cnt_ref[...].astype(jnp.float32), (8, blocks)), spread, NN, HIGHEST)[0:1]
    rows = mm(jnp.broadcast_to(rows_ref[...].astype(jnp.float32), (8, blocks)), spread, NN, HIGHEST)[0:1]
    precisions = jnp.where(slot < counts - 0.5, precisions, 0.0)
    local = lax.broadcasted_iota(jnp.int32, (half * crow, flat), 0) + e * (half * crow)
    reads = (jnp.abs(rows - local.astype(jnp.float32)) < 0.5).astype(jnp.float32)

    for i in range(half):
        @pl.when(has_down)
        def _():
            h_up[i].wait_recv()

        @pl.when(has_up)
        def _():
            h_down[i].wait_recv()

        for at in range(3):
            wide[at, i, crow : crow + 4] = h_after[i, at]
            wide[at, i, crow + 4 : crow + 8] = h_before[i, at]
        wl, wt = wide[1, i], wide[2, i]
        wl2, wt2 = wl * wl, wt * wt
        coef[i, 0] = 1.0 - wl2 - wt2
        coef[i, 1] = 0.5 * (wl2 - wl)
        coef[i, 2] = 0.5 * (wl2 + wl)
        coef[i, 3] = 0.5 * (wt2 - wt)
        coef[i, 4] = 0.5 * (wt2 + wt)
        for _ in range(STEPS):
            f = wide[0, i]
            wide[0, i] = (
                coef[i, 0] * f
                + coef[i, 1] * turn(f, -1, 1)
                + coef[i, 2] * turn(f, 1, 1)
                + coef[i, 3] * turn(f, -1, 0)
                + coef[i, 4] * turn(f, 1, 0)
            )
        end_v[i] = wide[0, i, 0:crow]

        @pl.when(has_later & (i < half // 2))
        def _():
            e_copy[i].start()

    fhi, flo = split(jnp.concatenate([end_v[i] for i in range(half)], axis=0))
    jh, jl = jhi[...], jlo[...]
    rows_own = half * crow
    both = mm(jnp.concatenate([fhi, flo], axis=0), jh, NT)
    seen = both[:rows_own] + both[rows_own:] + mm(fhi, jl, NT)
    evolved = jnp.sum(seen * reads, axis=0, keepdims=True)
    whi, wlo = split(reads * (precisions * (evolved - values)))
    both = mm(jnp.concatenate([whi, wlo], axis=0), jh, NN)
    placed = both[:rows_own] + both[rows_own:] + mm(whi, jl, NN)

    @pl.when(has_later)
    def _():
        n_copy.wait_recv()

    @pl.when(jnp.logical_not(has_later))
    def _():
        for i in range(half):
            nxt_v[i] = end_v[i, :, 0:lon]

    for i in range(half):
        prec = mp_ref[e * half + i]
        later = prec * (nxt_v[i] - end_v[i, :, 0:lon])
        adj[i, 0:crow, 0:lon] = placed[i * crow : (i + 1) * crow, 0:lon] - later
        extend(adj, (i,), lon)
        adj[i, crow : crow + 8] = jnp.zeros((8, width), jnp.float32)

    def back(i):
        g = adj[i]
        return (
            coef[i, 0] * g
            + turn(coef[i, 1] * g, 1, 1)
            + turn(coef[i, 2] * g, -1, 1)
            + turn(coef[i, 3] * g, 1, 0)
            + turn(coef[i, 4] * g, -1, 0)
        )

    def owner_copy(i, h):
        return remote(
            forc.at[i, h], rs_v.at[k], rs_ssem.at[i, h], rs_rsem.at[k], {"tm": e * half + i, "ens": h}
        )

    def edge_copy(i, h, device):
        return remote(edge.at[i, h], edge_v.at[k], ed_ssem.at[i, h], ed_rsem.at[k], device)

    edge_up = [edge_copy(i, 0, {"tm": e * half + i, "lat": lax.rem(b + 1, L), "ens": 0}) for i in range(half)]
    edge_down = [
        edge_copy(i, 1, {"tm": e * half + i, "lat": lax.rem(b + L - 1, L), "ens": E - 1}) for i in range(half)
    ]

    for i in range(half):
        for h in range(E):
            forc[i, h] = adj[i, h * 8 : h * 8 + 8]
        rim = jnp.zeros((8, width), jnp.float32)
        for _ in range(STEPS - 1):
            adj[i] = back(i)
            for h in range(E):
                forc[i, h] += adj[i, h * 8 : h * 8 + 8]
            rim = rim + adj[i, crow : crow + 8]
        edge[i, 0] = rim[0:4]
        edge[i, 1] = rim[4:8]

        @pl.when(has_up)
        def _():
            edge_up[i].start()

        @pl.when(has_down)
        def _():
            edge_down[i].start()

        for h in range(E):
            here = (k == e * half + i) & (e == h)

            @pl.when(here)
            def _():
                rs_v[k] = forc[i, h]

            @pl.when(jnp.logical_not(here))
            def _():
                owner_copy(i, h).start()

    for i in range(half):
        adj[i] = back(i)
        a_up_v[i] = adj[i, crow : crow + 4]
        a_down_v[i] = adj[i, crow + 4 : crow + 8]
    a_up = remote(a_up_v, a_before, a_ssem.at[0], a_rsem.at[0], up)
    a_down = remote(a_down_v, a_after, a_ssem.at[1], a_rsem.at[1], down)

    @pl.when(has_up)
    def _():
        a_up.start()

    @pl.when(has_down)
    def _():
        a_down.start()

    for i in range(half):
        for h in range(E):
            here = (k == e * half + i) & (e == h)

            @pl.when(jnp.logical_not(here))
            def _():
                owner_copy(i, h).wait_send()

    @pl.when(has_later)
    def _():
        for i in range(half // 2, half):
            e_copy[i].start()

    p_copy.wait_recv()
    for at in range(T):
        inside = (k == at) & (e == at // half)

        @pl.when(jnp.logical_not(inside))
        def _():
            remote(forc.at[0, 0], rs_v.at[at], rs_ssem.at[0, 0], rs_rsem.at[at], partner).wait_recv()

    @pl.when(edge_in)
    def _():
        for at in range(T):
            remote(edge.at[0, 0], edge_v.at[at], ed_ssem.at[0, 0], ed_rsem.at[at], partner).wait_recv()

    total, rim = rs_v[0], edge_v[0]
    for at in range(1, T):
        total = total + rs_v[at]
        rim = rim + edge_v[at]
    line = lax.broadcasted_iota(jnp.int32, (8, width), 0)
    rim = jnp.concatenate([rim, rim], axis=0)
    total = total + jnp.where((line < 4) == (e == 0), rim, 0.0)
    total = total[:, 0:lon]
    lane = lax.broadcasted_iota(jnp.int32, (8, 128), 1)
    part = jnp.zeros((8, 128), jnp.float32)
    for m in range(E * members):
        dots = jnp.sum(pert_v[m // members, m % members, e] * total, axis=1, keepdims=True)
        part = jnp.where(lane == m, dots, part)
    part = jnp.sum(part, axis=0, keepdims=True)
    ca_send[...] = part
    if direct:
        crowd = [(dt, db, de) for dt in range(T) for db in range(L) for de in range(E) if dt or db or de]
        pl.semaphore_wait(all_sem, L - 1)
    else:
        crowd = [(dt, 0, de) for dt, de in group]

    def seat(dt, db, de):
        at, lat, ens = lax.rem(k + dt, T), lax.rem(b + db, L), lax.rem(e + de, E)
        index = (at * L + lat) * E + ens if direct else at * E + ens
        return index, {"tm": at, "lat": lat, "ens": ens}

    sums = cb_v if direct else ca_v
    me, _ = seat(0, 0, 0)
    sums[me] = part
    coef_copies = []
    for at, (dt, db, de) in enumerate(crowd):
        copy = remote(ca_send, sums.at[me], ca_ssem.at[at], ca_rsem.at[me], seat(dt, db, de)[1])
        copy.start()
        coef_copies.append(copy)

    @pl.when(has_prior)
    def _():
        for i in range(half):
            e_copy[i].wait_recv()

    @pl.when(has_down)
    def _():
        a_up.wait_recv()

    @pl.when(has_up)
    def _():
        a_down.wait_recv()

    for i in range(half):
        prec = mp_ref[e * half + i]
        gap = jnp.zeros((crow - 8, lon), jnp.float32)
        rims = jnp.concatenate([a_before[i][:, 0:lon], gap, a_after[i][:, 0:lon]], axis=0)
        grad_v[e * half + i] = adj[i, 0:crow, 0:lon] + rims + prec * (inc_v[i] - prior_v[i, :, 0:lon])
    g_copy = remote(grad_v.at[own], grad_v.at[own], g_ssem, g_rsem, partner)
    g_copy.start()
    for dt, db, de in crowd:
        it, _ = seat(dt, db, de)
        remote(ca_send, sums.at[it], ca_ssem.at[0], ca_rsem.at[it], partner).wait_recv()
    if not direct:
        part = ca_v[0]
        for at in range(1, T * E):
            part = part + ca_v[at]
        cb_send[...] = part
        cb_v[b] = part
        for db in range(1, L):
            copy = remote(cb_send, cb_v.at[b], cb_ssem.at[db], cb_rsem.at[b], {"lat": lax.rem(b + db, L)})
            copy.start()
            coef_copies.append(copy)
        for db in range(1, L):
            it = lax.rem(b + db, L)
            remote(cb_send, cb_v.at[it], cb_ssem.at[0], cb_rsem.at[it], partner).wait_recv()
    g_copy.wait_recv()

    @pl.when(has_up)
    def _():
        for i in range(half):
            h_up[i].wait_send()
        a_up.wait_send()

    @pl.when(has_down)
    def _():
        for i in range(half):
            h_down[i].wait_send()
        a_down.wait_send()

    @pl.when(has_prior)
    def _():
        n_copy.wait_send()

    @pl.when(has_later)
    def _():
        for i in range(half):
            e_copy[i].wait_send()

    p_copy.wait_send()
    g_copy.wait_send()
    for i in range(half):
        @pl.when(has_up)
        def _():
            edge_up[i].wait_send()

        @pl.when(has_down)
        def _():
            edge_down[i].wait_send()

    for copy in coef_copies:
        copy.wait_send()


def finish(grad_v, pert_v, cb_v, grad_hbm, step_hbm, step_v, out_sem):
    g_out = pltpu.make_async_copy(grad_v, grad_hbm, out_sem.at[0])
    g_out.start()
    ens, members, rows, _, lon = pert_v.shape
    count = ens * members
    part = cb_v[0]
    for at in range(1, cb_v.shape[0]):
        part = part + cb_v[at]
    factor = jnp.broadcast_to(part, (8, 128)) * (-1.0 / (count - 1.0))
    for h in range(rows):
        mixed = jnp.zeros((8, lon), jnp.float32)
        for m in range(count):
            mixed = mixed + factor[:, m : m + 1] * pert_v[m // members, m % members, h]
        step_v[h * 8 : h * 8 + 8, :] = mixed
    s_out = pltpu.make_async_copy(step_v, step_hbm, out_sem.at[1])
    s_out.start()
    g_out.wait()
    s_out.wait()


def on_device(T, L, E, increment, wind_lon, wind_lat, model_precision, perturbations, obs_rows, obs_jacobian,
              obs_values, obs_precision, obs_counts):
    _, levels, crow, lon = increment.shape
    members = perturbations.shape[0]
    blocks, slots = obs_jacobian.shape[1:3]
    half, width = levels // E, -(-lon // 128) * 128
    flat = blocks * slots
    heard, spoken = (T * L * E, T * L * E) if T * L * E <= 64 else (L, T * E)
    f32, dma = jnp.float32, pltpu.SemaphoreType.DMA
    vmem, anyw = pl.BlockSpec(memory_space=pltpu.VMEM), pl.BlockSpec(memory_space=pl.ANY)

    def buf(*shape, kind=f32):
        return pltpu.VMEM(shape, kind)

    parts = pl.pallas_call(
        functools.partial(kernel, T, L, E),
        out_shape=(
            buf(levels, crow, lon),
            buf(E, members, crow // 8, 8, lon),
            buf(heard, 1, 128),
        ),
        in_specs=[pl.BlockSpec(memory_space=pltpu.HBM)] * 10,
        out_specs=(vmem, vmem, vmem),
        scratch_shapes=[
            pltpu.VMEM((1, blocks), jnp.int32), pltpu.VMEM((1, blocks), jnp.int32),
            buf(slots, blocks), buf(slots, blocks), pltpu.SMEM((levels,), f32),
            buf(half, crow, lon), buf(half, crow, lon), buf(half, crow, lon),
            buf(flat, lon),
            buf(flat, width, kind=jnp.bfloat16), buf(flat, width, kind=jnp.bfloat16),
            buf(3, half, 24, width), buf(half, 5, 24, width), buf(half, 24, width),
            buf(half, 3, 4, width), buf(half, 3, 4, width), buf(half, 3, 4, width), buf(half, 3, 4, width),
            buf(half, 4, width), buf(half, 4, width), buf(half, 4, width), buf(half, 4, width),
            buf(half, crow, width), buf(half, crow, lon), buf(half, crow, width),
            buf(half, E, 8, width), buf(half, 2, 4, width), buf(T, 8, width), buf(T, 4, width),
            buf(1, 128), buf(T * E, 1, 128), buf(1, 128),
            dma((10,)), dma((2, half)), dma((2, half)), dma((2,)), dma((2,)), dma((1,)), dma((1,)),
            dma((half,)), dma((half,)), dma, dma,
            dma((half, E)), dma((T,)), dma((half, 2)), dma((T,)),
            dma((spoken,)), dma((spoken,)), dma((L,)), dma((L,)), dma, dma, pltpu.SemaphoreType.REGULAR,
        ],
        compiler_params=pltpu.CompilerParams(
            collective_id=0, has_side_effects=True, vmem_limit_bytes=56 * 1024 * 1024
        ),
    )(
        obs_rows, obs_counts, obs_values[0].T, obs_precision[0].T, model_precision,
        increment[0], wind_lon[0], wind_lat[0],
        obs_jacobian.reshape(flat, lon),
        perturbations.reshape(members, crow // 8, 8, lon),
    )
    grad, step = pl.pallas_call(
        finish,
        out_shape=(
            jax.ShapeDtypeStruct((levels, crow, lon), f32),
            jax.ShapeDtypeStruct((crow, lon), f32),
        ),
        in_specs=[vmem] * 3,
        out_specs=(anyw, anyw),
        scratch_shapes=[buf(crow, lon), dma((2,))],
        compiler_params=pltpu.CompilerParams(vmem_limit_bytes=8 * 1024 * 1024),
    )(*[pltpu.with_memory_space_constraint(item, pltpu.VMEM) for item in parts])
    return grad[None], step[None]


def solution(mesh):
    T, L, E = mesh.shape["tm"], mesh.shape["lat"], mesh.shape["ens"]
    placed = (
        P("tm", None, "lat", None),
        P("tm", None, "lat", None),
        P("tm", None, "lat", None),
        P(),
        P("ens", "tm", "lat", None),
        P("tm", "lat"),
        P("tm", "lat", None, None),
        P("tm", "lat", None),
        P("tm", "lat", None),
        P("tm", "lat"),
    )
    return jax.shard_map(
        functools.partial(on_device, T, L, E),
        mesh=mesh,
        in_specs=placed,
        out_specs=(P("tm", None, "lat", None), P("tm", "lat", None)),
        check_vma=False,
    )
```

profile of v0, /device:TPU:0, one launch (start us, length us, event | category | flops | bytes accessed | tf_op | source)
XLA Modules:
  0.0 25.0 jit_solution(12748324928047681941)
XLA Ops:
  0.6 23.4 %shard_map.113 = (f32[4,16,1440]{2,1,0:T(8,128)S(1)}, f32[2,16,2,8,1440]{4,3,2,1,0:T(8,128)S(1)}, f32[32,1,128]{2,1,0:T(1,128)S(1)}) custom-call(s32[1,32]{1,0:T(1,128)} %rows_hbm.1, s32[1,32]{1,0:T(1,128)} %cnt_hbm.1, f32[16,32]{1,0:T(8,128)} %bitcast.18, f32[16,32]{1,0:T(8,128)} %bitcast.19, f32[4]{0:T(128)} %mp_hbm.1, f32[4,16,1440]{2,1,0:T(8,128)} %bitcast.15, ...), custom_call_target="tpu_custom_call" | custom-call | tf_op jit(solution)/shard_map/pallas_call | solution.py:493
  24.1 1.0 %shard_map.114 = (f32[4,16,1440]{2,1,0:T(8,128)}, f32[16,1440]{1,0:T(8,128)}) custom-call(f32[4,16,1440]{2,1,0:T(8,128)S(1)} %get-tuple-element.7.grad_v, f32[2,16,2,8,1440]{4,3,2,1,0:T(8,128)S(1)} %get-tuple-element.8.pert_v, f32[32,1,128]{2,1,0:T(1,128)S(1)} %get-tuple-element.9.cb_v), custom_call_target="tpu_custom_call" | custom-call | tf_op jit(solution)/shard_map/pallas_call | solution.py:528
where the time goes:
time: 25.2 us; the launch traced here: 25 us
  Pallas kernels  24.4 us (97%)
  between operations  0.64 us (3%)
    pallas_call x1, Pallas kernels, on_device(): pl.pallas_call(functools.partial(kernel, T, L, E), out_shape=(buf(levels,...  23.4 us
    pallas_call x1, Pallas kernels, on_device(): pl.pallas_call(finish, out_shape=(jax.ShapeDtypeStruct((levels, crow, lon...  0.97 us

commit v1 on v0

v1 whole, which is shorter than its diff:
```python
import functools

import jax
import jax.numpy as jnp
from jax import lax
from jax.experimental import pallas as pl
from jax.experimental.pallas import tpu as pltpu
from jax.sharding import PartitionSpec as P

STEPS = 4
MESH = pl.DeviceIdType.MESH
HIGHEST = lax.Precision.HIGHEST
NN = (((1,), (0,)), ((), ()))


def mm(a, b, dims, precision=None):
    return lax.dot_general(a, b, dims, precision=precision, preferred_element_type=jnp.float32)


def split(value):
    hi = value.astype(jnp.bfloat16)
    lo = (value - hi.astype(jnp.float32)).astype(jnp.bfloat16)
    return hi, lo


def turn(value, steps, axis):
    return pltpu.roll(value, steps % value.shape[axis], axis)


def extend(ref, where, lon):
    width = ref.shape[-1]
    rem = lon % 128
    last = ref[where + (slice(0, 16), slice(width - 128, width))]
    before = ref[where + (slice(0, 16), slice(width - 256, width - 128))]
    first = ref[where + (slice(0, 16), slice(0, 128))]
    lane = lax.broadcasted_iota(jnp.int32, last.shape, 1)
    wrapped = jnp.where(lane < 128 - rem, turn(before, 128 - rem, 1), turn(last, 128 - rem, 1))
    right = jnp.where(lane < rem + (128 - rem) // 2, turn(first, rem, 1), wrapped)
    ref[where + (slice(0, 16), slice(width - 128, width))] = jnp.where(lane < rem, last, right)


def kernel(
    T, L, E,
    rows_hbm, cnt_hbm, val_hbm, prc_hbm, mp_hbm, inc_hbm, wlon_hbm, wlat_hbm, jac_hbm, pert_hbm,
    grad_v, pert_v, cb_v,
    rows_s, rows_ref, cnt_ref, val_ref, prc_ref, mp_ref, fields, jac_v, tail, val_b, prc_b, part_v, wgt, pick,
    wide, coef, adj, h_first, h_last, h_after, h_before, a_up_v, a_down_v, a_after, a_before,
    end_v, lines, nxt_v, prior_v, forc, edge, rs_v, edge_v, ca_send, ca_v, cb_send,
    load_sem, small_sem, h_ssem, h_rsem, a_ssem, a_rsem, t_ssem, t_rsem, e_ssem, e_rsem, p_ssem, p_rsem,
    rs_ssem, rs_rsem, ed_ssem, ed_rsem, ca_ssem, ca_rsem, cb_ssem, cb_rsem, g_ssem, g_rsem, all_sem,
):
    k, b, e = lax.axis_index("tm"), lax.axis_index("lat"), lax.axis_index("ens")
    _, half, crow, lon = fields.shape
    width = wide.shape[-1]
    members = pert_v.shape[1]
    slots, blocks = val_ref.shape
    tiles, rem = width // 128, lon % 128
    other = 1 - e
    own = pl.ds(e * half, half)

    def shift(at):
        return lax.rem(at + at // 2 + 1 + e, half)

    def spot(t, at, there):
        return lax.rem(t + shift(at) + half - shift(there), half)

    order = [lax.rem(shift(k) + t, half) for t in range(half)]
    level = [e * half + at for at in order]

    def local(src, dst, sem):
        return pltpu.make_async_copy(src, dst, sem)

    for at, ref in enumerate((inc_hbm, wlon_hbm, wlat_hbm)):
        for t in range(half):
            local(ref.at[level[t]], fields.at[at, t], load_sem.at[0]).start()
    small = [
        local(rows_hbm, rows_s, small_sem.at[0]),
        local(rows_hbm, rows_ref, small_sem.at[1]),
        local(cnt_hbm, cnt_ref, small_sem.at[2]),
        local(val_hbm, val_ref, small_sem.at[3]),
        local(prc_hbm, prc_ref, small_sem.at[4]),
        local(mp_hbm, mp_ref, small_sem.at[5]),
    ]

    barrier = pltpu.get_barrier_semaphore()
    direct = T * L * E <= 64
    group = [(dt, de) for dt in range(T) for de in range(E) if dt or de]

    def mate(dt, de):
        return {"tm": lax.rem(k + dt, T), "ens": lax.rem(e + de, E)}

    for dt, de in group:
        pl.semaphore_signal(barrier, inc=1, device_id=mate(dt, de), device_id_type=MESH)
    for db in range(1, L):
        pl.semaphore_signal(barrier, inc=1, device_id={"lat": lax.rem(b + db, L)}, device_id_type=MESH)

    def remote(src, dst, ssem, rsem, device):
        return pltpu.make_async_remote_copy(
            src_ref=src, dst_ref=dst, send_sem=ssem, recv_sem=rsem, device_id=device, device_id_type=MESH
        )

    up = {"lat": lax.rem(b + 1, L)}
    down = {"lat": lax.rem(b + L - 1, L)}
    later_k, prior_k = lax.rem(k + 1, T), lax.rem(k + T - 1, T)
    partner = {"ens": other}
    has_up, has_down = b < L - 1, b > 0
    has_later, has_prior = k < T - 1, k > 0

    local(fields, fields, load_sem.at[0]).wait()
    jac_load = local(jac_hbm, jac_v, load_sem.at[1])
    pert_load = local(pert_hbm, pert_v.at[e], load_sem.at[2])
    for item in small + [pert_load, jac_load]:
        item.start()
    for t in range(half):
        for at in range(3):
            wide[at, t, 0:16, 0:lon] = fields[at, t]
            extend(wide, (at, t), lon)
        h_first[t, 0] = wide[0, t, 0:2]
        h_first[t, 1] = wide[0, t, 2:4]
        h_last[t, 0] = wide[0, t, crow - 4 : crow - 2]
        h_last[t, 1] = wide[0, t, crow - 2 : crow]
        for at in (1, 2):
            h_first[t, 1 + at] = wide[at, t, 0:2]
            h_first[t, 4, at - 1 : at] = wide[at, t, 2:3]
            h_last[t, 1 + at] = wide[at, t, crow - 2 : crow]
            h_last[t, 4, at - 1 : at] = wide[at, t, crow - 3 : crow - 2]

    pl.semaphore_wait(barrier, len(group) + L - 1)
    if direct:
        for db in range(1, L):
            pl.semaphore_signal(all_sem, inc=1, device_id={"lat": lax.rem(b + db, L)}, device_id_type=MESH)

    h_up = [remote(h_last.at[t], h_before.at[t], h_ssem.at[0], h_rsem.at[0, t], up) for t in range(half)]
    h_down = [remote(h_first.at[t], h_after.at[t], h_ssem.at[1], h_rsem.at[1, t], down) for t in range(half)]
    n_copy = [
        remote(fields.at[0, spot(t, prior_k, k)], nxt_v.at[t], t_ssem, t_rsem.at[t], {"tm": prior_k})
        for t in range(half)
    ]

    def e_copy(t):
        there = spot(t, k, later_k)
        return remote(end_v.at[t], prior_v.at[there], e_ssem, e_rsem.at[there], {"tm": later_k})

    for t in range(half):
        @pl.when(has_up)
        def _():
            h_up[t].start()

        @pl.when(has_down)
        def _():
            h_down[t].start()

        @pl.when(has_prior)
        def _():
            n_copy[t].start()

    pert_load.wait()
    p_copy = remote(pert_v.at[e], pert_v.at[e], p_ssem, p_rsem, partner)
    p_copy.start()

    @pl.when(jnp.logical_not(has_up))
    def _():
        h_after[...] = jnp.zeros_like(h_after)
        a_after[...] = jnp.zeros_like(a_after)

    @pl.when(jnp.logical_not(has_down))
    def _():
        h_before[...] = jnp.zeros_like(h_before)
        a_before[...] = jnp.zeros_like(a_before)

    @pl.when(jnp.logical_not(has_prior))
    def _():
        prior_v[...] = jnp.zeros_like(prior_v)

    @pl.when(jnp.logical_not(has_later))
    def _():
        nxt_v[...] = jnp.zeros_like(nxt_v)

    edge_in = ((e == 0) & has_down) | ((e == E - 1) & has_up)

    @pl.when(jnp.logical_not(edge_in))
    def _():
        edge_v[...] = jnp.zeros_like(edge_v)

    def weigh(t, rows):
        wl, wt = wide[1, t, rows], wide[2, t, rows]
        wl2, wt2 = wl * wl, wt * wt
        coef[t, 0, rows] = 1.0 - wl2 - wt2
        coef[t, 1, rows] = 0.5 * (wl2 - wl)
        coef[t, 2, rows] = 0.5 * (wl2 + wl)
        coef[t, 3, rows] = 0.5 * (wt2 - wt)
        coef[t, 4, rows] = 0.5 * (wt2 + wt)

    for t in range(half):
        weigh(t, slice(0, crow))
        for at in (1, 2):
            wide[at, t, crow : crow + 8] = jnp.zeros((8, width), jnp.float32)

    for item in small:
        item.wait()
    deep = lax.broadcasted_iota(jnp.int32, (slots, blocks), 0)
    precisions = jnp.where(deep < cnt_ref[...], prc_ref[...], 0.0)
    values = val_ref[...]
    for j in range(blocks):
        prc_b[j] = jnp.broadcast_to(precisions[:, j : j + 1], (slots, 128)).reshape(slots // 8, 8, 128)
        val_b[j] = jnp.broadcast_to(values[:, j : j + 1], (slots, 128)).reshape(slots // 8, 8, 128)
    column = lax.broadcasted_iota(jnp.int32, (blocks, blocks * 8), 1)
    block = lax.broadcasted_iota(jnp.int32, (blocks, blocks * 8), 0)
    spread = ((column >= block * 8) & (column < (block + 1) * 8)).astype(jnp.float32)
    rows = mm(jnp.broadcast_to(rows_ref[...].astype(jnp.float32), (8, blocks)), spread, NN, HIGHEST)[0:1]
    line = lax.broadcasted_iota(jnp.int32, (crow, blocks * 8), 0)
    for t in range(half):
        wanted = (line + level[t] * crow).astype(jnp.float32)
        pick[t] = (jnp.abs(rows - wanted) < 0.5).astype(jnp.bfloat16)

    jac_load.wait()
    if rem:
        tail[...] = jnp.zeros_like(tail)
        tail[:, :, :, 0:rem] = jac_v[:, :, :, lon - rem : lon]

    def strip(at, c):
        if rem and c == tiles - 1:
            return tail[at]
        return jac_v[at, :, :, c * 128 : (c + 1) * 128]

    def observe(t):
        def measure(base, carry):
            for u in range(4):
                j = base * 4 + u
                row = lax.rem(rows_s[0, j], crow)
                total = jnp.zeros((slots // 8, 8, 128), jnp.float32)
                for c in range(tiles):
                    total = total + strip(j, c) * lines[row, :, c * 128 : (c + 1) * 128]
                part_v[j] = total
            return carry

        lax.fori_loop(0, blocks // 4, measure, 0)
        evolved = jnp.sum(part_v[...], axis=-1, keepdims=True)
        wgt[...] = prc_b[...] * (evolved - val_b[...])
        for c in range(0, tiles, 2):
            pieces = []
            for cc in range(c, min(c + 2, tiles)):
                piece = jnp.sum(strip(slice(None), cc) * wgt[...], axis=1)
                pieces.append(piece.reshape(blocks * 8, 128))
            hi, lo = split(jnp.concatenate(pieces, axis=1))
            adj[t, 0:crow, c * 128 : c * 128 + hi.shape[1]] = mm(pick[t], hi, NN) + mm(pick[t], lo, NN)

    def back(t):
        g = adj[t]
        return (
            coef[t, 0] * g
            + turn(coef[t, 1] * g, 1, 1)
            + turn(coef[t, 2] * g, -1, 1)
            + turn(coef[t, 3] * g, 1, 0)
            + turn(coef[t, 4] * g, -1, 0)
        )

    def owner_copy(t, h):
        return remote(forc.at[t * E + h], rs_v.at[k], rs_ssem, rs_rsem, {"tm": level[t], "ens": h})

    def edge_copy(t, h, device):
        return remote(edge.at[h, t], edge_v.at[k], ed_ssem.at[h], ed_rsem, device)

    edge_up = [edge_copy(t, 0, {"tm": level[t], "lat": lax.rem(b + 1, L), "ens": 0}) for t in range(half)]
    edge_down = [edge_copy(t, 1, {"tm": level[t], "lat": lax.rem(b + L - 1, L), "ens": E - 1}) for t in range(half)]

    for t in range(half):
        @pl.when(has_down)
        def _():
            h_up[t].wait_recv()

        @pl.when(has_up)
        def _():
            h_down[t].wait_recv()

        wide[0, t, crow : crow + 2] = h_after[t, 0]
        wide[0, t, crow + 2 : crow + 4] = h_after[t, 1]
        wide[0, t, crow + 4 : crow + 6] = h_before[t, 0]
        wide[0, t, crow + 6 : crow + 8] = h_before[t, 1]
        for at in (1, 2):
            wide[at, t, crow : crow + 2] = h_after[t, 1 + at]
            wide[at, t, crow + 2 : crow + 3] = h_after[t, 4, at - 1 : at]
            wide[at, t, crow + 5 : crow + 6] = h_before[t, 4, at - 1 : at]
            wide[at, t, crow + 6 : crow + 8] = h_before[t, 1 + at]
        weigh(t, slice(crow, crow + 8))
        for _ in range(STEPS):
            f = wide[0, t]
            wide[0, t] = (
                coef[t, 0] * f
                + coef[t, 1] * turn(f, -1, 1)
                + coef[t, 2] * turn(f, 1, 1)
                + coef[t, 3] * turn(f, -1, 0)
                + coef[t, 4] * turn(f, 1, 0)
            )
        end_v[t] = wide[0, t, 0:crow]
        for r in range(crow):
            lines[r] = wide[0, t, r : r + 1]
        observe(t)
        @pl.when(has_later)
        def _():
            n_copy[t].wait_recv()

        scale = jnp.where(has_later, mp_ref[level[t]], 0.0)
        adj[t, 0:crow, 0:lon] = adj[t, 0:crow, 0:lon] - scale * (nxt_v[t] - end_v[t, :, 0:lon])
        extend(adj, (t,), lon)
        adj[t, crow : crow + 8] = jnp.zeros((8, width), jnp.float32)
        for h in range(E):
            forc[t * E + h] = adj[t, h * 8 : h * 8 + 8]
        rim = jnp.zeros((8, width), jnp.float32)
        for _ in range(STEPS - 1):
            adj[t] = back(t)
            for h in range(E):
                forc[t * E + h] += adj[t, h * 8 : h * 8 + 8]
            rim = rim + adj[t, crow : crow + 8]
        edge[0, t] = rim[0:4]
        edge[1, t] = rim[4:8]

        @pl.when(has_up)
        def _():
            edge_up[t].start()

        @pl.when(has_down)
        def _():
            edge_down[t].start()

        for h in range(E):
            here = (k == level[t]) & (e == h)

            @pl.when(here)
            def _():
                rs_v[k] = forc[t * E + h]

            @pl.when(jnp.logical_not(here))
            def _():
                owner_copy(t, h).start()

    for t in range(half):
        adj[t] = back(t)
        a_up_v[t] = adj[t, crow : crow + 4]
        a_down_v[t] = adj[t, crow + 4 : crow + 8]
    a_up = remote(a_up_v, a_before, a_ssem.at[0], a_rsem.at[0], up)
    a_down = remote(a_down_v, a_after, a_ssem.at[1], a_rsem.at[1], down)

    @pl.when(has_up)
    def _():
        a_up.start()

    @pl.when(has_down)
    def _():
        a_down.start()

    owner = k // half == e

    def all_but(ref, some):
        return ref.at[pl.ds(0, ref.shape[0] - some)]

    for some, when in ((1, owner), (0, jnp.logical_not(owner))):
        @pl.when(when)
        def _():
            remote(all_but(forc, some), all_but(forc, some), rs_ssem, rs_rsem, partner).wait_send()

    @pl.when(has_later)
    def _():
        for t in range(half):
            e_copy(t).start()

    p_copy.wait_recv()
    for some, when in ((1, owner), (0, jnp.logical_not(owner))):
        @pl.when(when)
        def _():
            remote(all_but(rs_v, some), all_but(rs_v, some), rs_ssem, rs_rsem, partner).wait_recv()

    @pl.when(edge_in)
    def _():
        remote(edge_v, edge_v, ed_ssem.at[0], ed_rsem, partner).wait_recv()

    total, rim = rs_v[0], edge_v[0]
    for at in range(1, T):
        total = total + rs_v[at]
        rim = rim + edge_v[at]
    line = lax.broadcasted_iota(jnp.int32, (8, width), 0)
    rim = jnp.concatenate([rim, rim], axis=0)
    total = total + jnp.where((line < 4) == (e == 0), rim, 0.0)
    total = total[:, 0:lon]
    lane = lax.broadcasted_iota(jnp.int32, (8, 128), 1)
    part = jnp.zeros((8, 128), jnp.float32)
    for m in range(E * members):
        dots = jnp.sum(pert_v[m // members, m % members, e] * total, axis=1, keepdims=True)
        part = jnp.where(lane == m, dots, part)
    part = jnp.sum(part, axis=0, keepdims=True)
    ca_send[...] = part
    if direct:
        crowd = [(dt, db, de) for dt in range(T) for db in range(L) for de in range(E) if dt or db or de]
        pl.semaphore_wait(all_sem, L - 1)
    else:
        crowd = [(dt, 0, de) for dt, de in group]

    def seat(dt, db, de):
        at, lat, ens = lax.rem(k + dt, T), lax.rem(b + db, L), lax.rem(e + de, E)
        index = (at * L + lat) * E + ens if direct else at * E + ens
        return index, {"tm": at, "lat": lat, "ens": ens}

    sums = cb_v if direct else ca_v
    me, _ = seat(0, 0, 0)
    sums[me] = part
    for dt, db, de in crowd:
        remote(ca_send, sums.at[me], ca_ssem, ca_rsem, seat(dt, db, de)[1]).start()

    @pl.when(has_prior)
    def _():
        for t in range(half):
            remote(end_v.at[t], prior_v.at[t], e_ssem, e_rsem.at[t], partner).wait_recv()

    @pl.when(has_down)
    def _():
        a_up.wait_recv()

    @pl.when(has_up)
    def _():
        a_down.wait_recv()

    for t in range(half):
        prec = mp_ref[level[t]]
        gap = jnp.zeros((crow - 8, lon), jnp.float32)
        rims = jnp.concatenate([a_before[t][:, 0:lon], gap, a_after[t][:, 0:lon]], axis=0)
        grad_v[level[t]] = adj[t, 0:crow, 0:lon] + rims + prec * (fields[0, t] - prior_v[t, :, 0:lon])
    g_copy = remote(grad_v.at[own], grad_v.at[own], g_ssem, g_rsem, partner)
    g_copy.start()
    others = sums.at[pl.ds(0, len(crowd))]
    remote(others, others, ca_ssem, ca_rsem, partner).wait_recv()
    if not direct:
        part = ca_v[0]
        for at in range(1, T * E):
            part = part + ca_v[at]
        cb_send[...] = part
        cb_v[b] = part
        for db in range(1, L):
            remote(cb_send, cb_v.at[b], cb_ssem, cb_rsem, {"lat": lax.rem(b + db, L)}).start()
        bands = remote(all_but(cb_v, 1), all_but(cb_v, 1), cb_ssem, cb_rsem, partner)
        bands.wait_recv()
    g_copy.wait_recv()

    @pl.when(has_up)
    def _():
        remote(h_last, h_before, h_ssem.at[0], h_rsem.at[0, 0], up).wait_send()
        a_up.wait_send()
        remote(edge.at[0], edge.at[0], ed_ssem.at[0], ed_rsem, up).wait_send()

    @pl.when(has_down)
    def _():
        remote(h_first, h_after, h_ssem.at[1], h_rsem.at[1, 0], down).wait_send()
        a_down.wait_send()
        remote(edge.at[1], edge.at[1], ed_ssem.at[1], ed_rsem, down).wait_send()

    @pl.when(has_prior)
    def _():
        remote(nxt_v, nxt_v, t_ssem, t_rsem.at[0], partner).wait_send()

    @pl.when(has_later)
    def _():
        remote(end_v, end_v, e_ssem, e_rsem.at[0], partner).wait_send()

    p_copy.wait_send()
    g_copy.wait_send()
    remote(others, others, ca_ssem, ca_rsem, partner).wait_send()
    if not direct:
        bands.wait_send()


def finish(grad_v, pert_v, cb_v, grad_hbm, step_hbm, step_v, out_sem):
    g_out = pltpu.make_async_copy(grad_v, grad_hbm, out_sem.at[0])
    g_out.start()
    ens, members, rows, _, lon = pert_v.shape
    count = ens * members
    part = cb_v[0]
    for at in range(1, cb_v.shape[0]):
        part = part + cb_v[at]
    factor = jnp.broadcast_to(part, (8, 128)) * (-1.0 / (count - 1.0))
    for h in range(rows):
        mixed = jnp.zeros((8, lon), jnp.float32)
        for m in range(count):
            mixed = mixed + factor[:, m : m + 1] * pert_v[m // members, m % members, h]
        step_v[h * 8 : h * 8 + 8, :] = mixed
    s_out = pltpu.make_async_copy(step_v, step_hbm, out_sem.at[1])
    s_out.start()
    g_out.wait()
    s_out.wait()


def on_device(T, L, E, increment, wind_lon, wind_lat, model_precision, perturbations, obs_rows, obs_jacobian,
              obs_values, obs_precision, obs_counts):
    _, levels, crow, lon = increment.shape
    members = perturbations.shape[0]
    blocks, slots = obs_jacobian.shape[1:3]
    half, width = levels // E, -(-lon // 128) * 128
    heard = T * L * E if T * L * E <= 64 else L
    f32, dma = jnp.float32, pltpu.SemaphoreType.DMA
    vmem, anyw = pl.BlockSpec(memory_space=pltpu.VMEM), pl.BlockSpec(memory_space=pl.ANY)

    def buf(*shape, kind=f32):
        return pltpu.VMEM(shape, kind)

    table = buf(blocks, slots // 8, 8, 128)
    parts = pl.pallas_call(
        functools.partial(kernel, T, L, E),
        out_shape=(
            buf(levels, crow, lon),
            buf(E, members, crow // 8, 8, lon),
            buf(heard, 1, 128),
        ),
        in_specs=[pl.BlockSpec(memory_space=pltpu.HBM)] * 10,
        out_specs=(vmem, vmem, vmem),
        scratch_shapes=[
            pltpu.SMEM((1, blocks), jnp.int32), pltpu.VMEM((1, blocks), jnp.int32), pltpu.VMEM((1, blocks), jnp.int32),
            buf(slots, blocks), buf(slots, blocks), pltpu.SMEM((levels,), f32),
            buf(3, half, crow, lon), buf(blocks, slots // 8, 8, lon), table, table, table, table, table,
            buf(half, crow, blocks * 8, kind=jnp.bfloat16),
            buf(3, half, 24, width), buf(half, 5, 24, width), buf(half, 24, width),
            buf(half, 5, 2, width), buf(half, 5, 2, width), buf(half, 5, 2, width), buf(half, 5, 2, width),
            buf(half, 4, width), buf(half, 4, width), buf(half, 4, width), buf(half, 4, width),
            buf(half, crow, width), buf(crow, 1, width), buf(half, crow, lon), buf(half, crow, width),
            buf(half * E, 8, width), buf(2, half, 4, width), buf(T, 8, width), buf(T, 4, width),
            buf(1, 128), buf(T * E, 1, 128), buf(1, 128),
            dma((3,)), dma((6,)), dma((2,)), dma((2, half)), dma((2,)), dma((2,)), dma, dma((half,)), dma, dma((half,)),
            dma, dma, dma, dma, dma((2,)), dma, dma, dma, dma, dma, dma, dma, pltpu.SemaphoreType.REGULAR,
        ],
        compiler_params=pltpu.CompilerParams(
            collective_id=0, has_side_effects=True, vmem_limit_bytes=56 * 1024 * 1024
        ),
    )(
        obs_rows, obs_counts, obs_values[0].T, obs_precision[0].T, model_precision,
        increment[0], wind_lon[0], wind_lat[0],
        obs_jacobian.reshape(blocks, slots // 8, 8, lon),
        perturbations.reshape(members, crow // 8, 8, lon),
    )
    grad, step = pl.pallas_call(
        finish,
        out_shape=(
            jax.ShapeDtypeStruct((levels, crow, lon), f32),
            jax.ShapeDtypeStruct((crow, lon), f32),
        ),
        in_specs=[vmem] * 3,
        out_specs=(anyw, anyw),
        scratch_shapes=[buf(crow, lon), dma((2,))],
        compiler_params=pltpu.CompilerParams(vmem_limit_bytes=8 * 1024 * 1024),
    )(*[pltpu.with_memory_space_constraint(item, pltpu.VMEM) for item in parts])
    return grad[None], step[None]


def solution(mesh):
    T, L, E = mesh.shape["tm"], mesh.shape["lat"], mesh.shape["ens"]
    placed = (
        P("tm", None, "lat", None),
        P("tm", None, "lat", None),
        P("tm", None, "lat", None),
        P(),
        P("ens", "tm", "lat", None),
        P("tm", "lat"),
        P("tm", "lat", None, None),
        P("tm", "lat", None),
        P("tm", "lat", None),
        P("tm", "lat"),
    )
    return jax.shard_map(
        functools.partial(on_device, T, L, E),
        mesh=mesh,
        in_specs=placed,
        out_specs=(P("tm", None, "lat", None), P("tm", "lat", None)),
        check_vma=False,
    )
```

time: 25.2 us -> 24.2 us (0.960)
  Pallas kernels: 24.4 us -> 23.4 us
    pallas_call x1, Pallas kernels: 23.4 us -> 22.4 us  [on_device(): pl.pallas_call(functools.partial(kernel, T, L, E), out_shape=(buf(levels,...]
where the time goes in v1:
time: 24.2 us; the launch traced here: 24 us
  Pallas kernels  23.4 us (97%)
  between operations  0.64 us (3%)
    pallas_call x1, Pallas kernels, on_device(): pl.pallas_call(functools.partial(kernel, T, L, E), out_shape=(buf(levels,...  22.4 us
    pallas_call x1, Pallas kernels, on_device(): pl.pallas_call(finish, out_shape=(jax.ShapeDtypeStruct((levels, crow, lon...  0.97 us

profile of v1, /device:TPU:0, one launch (start us, length us, event | category | flops | bytes accessed | tf_op | source)
XLA Modules:
  0.0 24.0 jit_solution(11835643958436601636)
XLA Ops:
  0.6 22.4 %shard_map.113 = (f32[4,16,1440]{2,1,0:T(8,128)S(1)}, f32[2,16,2,8,1440]{4,3,2,1,0:T(8,128)S(1)}, f32[32,1,128]{2,1,0:T(1,128)S(1)}) custom-call(s32[1,32]{1,0:T(1,128)} %rows_hbm.1, s32[1,32]{1,0:T(1,128)} %cnt_hbm.1, f32[16,32]{1,0:T(8,128)} %bitcast.18, f32[16,32]{1,0:T(8,128)} %bitcast.19, f32[4]{0:T(128)} %mp_hbm.1, f32[4,16,1440]{2,1,0:T(8,128)} %bitcast.15, ...), custom_call_target="tpu_custom_call" | custom-call | tf_op jit(solution)/shard_map/pallas_call | solution.py:504
  23.1 1.0 %shard_map.114 = (f32[4,16,1440]{2,1,0:T(8,128)}, f32[16,1440]{1,0:T(8,128)}) custom-call(f32[4,16,1440]{2,1,0:T(8,128)S(1)} %get-tuple-element.7.grad_v, f32[2,16,2,8,1440]{4,3,2,1,0:T(8,128)S(1)} %get-tuple-element.8.pert_v, f32[32,1,128]{2,1,0:T(1,128)S(1)} %get-tuple-element.9.cb_v), custom_call_target="tpu_custom_call" | custom-call | tf_op jit(solution)/shard_map/pallas_call | solution.py:536

commit v2 on v1

--- a/solution.py
+++ b/solution.py
@@ -45,9 +45,9 @@
     grad_v, pert_v, cb_v,
     rows_s, rows_ref, cnt_ref, val_ref, prc_ref, mp_ref, fields, jac_v, tail, val_b, prc_b, part_v, wgt, pick,
     wide, coef, adj, h_first, h_last, h_after, h_before, a_up_v, a_down_v, a_after, a_before,
-    end_v, lines, nxt_v, prior_v, forc, edge, rs_v, edge_v, ca_send, ca_v, cb_send,
+    end_v, lines, last, rims, nxt_v, prior_v, forc, edge, rs_v, edge_v, ca_send, ca_v, cb_send,
     load_sem, small_sem, h_ssem, h_rsem, a_ssem, a_rsem, t_ssem, t_rsem, e_ssem, e_rsem, p_ssem, p_rsem,
-    rs_ssem, rs_rsem, ed_ssem, ed_rsem, ca_ssem, ca_rsem, cb_ssem, cb_rsem, g_ssem, g_rsem, all_sem,
+    rs_ssem, rs_rsem, ed_ssem, ed_rsem, ca_ssem, ca_rsem, cb_ssem, cb_rsem, g_ssem, g_rsem, all_sem, round_sem, pair_sem,
 ):
     k, b, e = lax.axis_index("tm"), lax.axis_index("lat"), lax.axis_index("ens")
     _, half, crow, lon = fields.shape
@@ -56,16 +56,15 @@
     slots, blocks = val_ref.shape
     tiles, rem = width // 128, lon % 128
     other = 1 - e
-    own = pl.ds(e * half, half)
 
     def shift(at):
-        return lax.rem(at + at // 2 + 1 + e, half)
+        return lax.rem(at + e + 1, half)
 
     def spot(t, at, there):
         return lax.rem(t + shift(at) + half - shift(there), half)
 
     order = [lax.rem(shift(k) + t, half) for t in range(half)]
-    level = [e * half + at for at in order]
+    level = [at * E + lax.rem(e + at, E) for at in order]
 
     def local(src, dst, sem):
         return pltpu.make_async_copy(src, dst, sem)
@@ -89,10 +88,42 @@
     def mate(dt, de):
         return {"tm": lax.rem(k + dt, T), "ens": lax.rem(e + de, E)}
 
-    for dt, de in group:
-        pl.semaphore_signal(barrier, inc=1, device_id=mate(dt, de), device_id_type=MESH)
-    for db in range(1, L):
-        pl.semaphore_signal(barrier, inc=1, device_id={"lat": lax.rem(b + db, L)}, device_id_type=MESH)
+    near = direct and T == 4 and E == 2
+    ring = [
+        ({"ens": 1 - e}, None),
+        ({"tm": k + 1 - 2 * lax.rem(k, 2)}, None),
+        ({"tm": lax.rem(k + 2, T)}, None),
+        ({"lat": lax.rem(b + 1, L)}, b < L - 1),
+        ({"lat": lax.rem(b + L - 1, L)}, b > 0),
+    ]
+    middle = (k == 1) | (k == 2)
+
+    def greet(sem, extra):
+        for device, when in ring + ([({"tm": T - 1 - k}, middle)] if extra else []):
+            if when is None:
+                pl.semaphore_signal(sem, inc=1, device_id=device, device_id_type=MESH)
+            else:
+                @pl.when(when)
+                def _():
+                    pl.semaphore_signal(sem, inc=1, device_id=device, device_id_type=MESH)
+
+    def meet(sem, extra):
+        count = 3 + (b < L - 1).astype(jnp.int32) + (b > 0).astype(jnp.int32)
+        pl.semaphore_wait(sem, count + middle.astype(jnp.int32) if extra else count)
+
+    def round_on(at):
+        if near:
+            meet(round_sem.at[at], False)
+            if at < 2:
+                greet(round_sem.at[at + 1], False)
+
+    if near:
+        greet(barrier, True)
+    else:
+        for dt, de in group:
+            pl.semaphore_signal(barrier, inc=1, device_id=mate(dt, de), device_id_type=MESH)
+        for db in range(1, L):
+            pl.semaphore_signal(barrier, inc=1, device_id={"lat": lax.rem(b + db, L)}, device_id_type=MESH)
 
     def remote(src, dst, ssem, rsem, device):
         return pltpu.make_async_remote_copy(
@@ -125,10 +156,13 @@
             h_last[t, 1 + at] = wide[at, t, crow - 2 : crow]
             h_last[t, 4, at - 1 : at] = wide[at, t, crow - 3 : crow - 2]
 
-    pl.semaphore_wait(barrier, len(group) + L - 1)
-    if direct:
-        for db in range(1, L):
-            pl.semaphore_signal(all_sem, inc=1, device_id={"lat": lax.rem(b + db, L)}, device_id_type=MESH)
+    if near:
+        meet(barrier, True)
+    else:
+        pl.semaphore_wait(barrier, len(group) + L - 1)
+        if direct:
+            for db in range(1, L):
+                pl.semaphore_signal(all_sem, inc=1, device_id={"lat": lax.rem(b + db, L)}, device_id_type=MESH)
 
     h_up = [remote(h_last.at[t], h_before.at[t], h_ssem.at[0], h_rsem.at[0, t], up) for t in range(half)]
     h_down = [remote(h_first.at[t], h_after.at[t], h_ssem.at[1], h_rsem.at[1, t], down) for t in range(half)]
@@ -154,6 +188,8 @@
         def _():
             n_copy[t].start()
 
+    if near:
+        greet(round_sem.at[0], False)
     pert_load.wait()
     p_copy = remote(pert_v.at[e], pert_v.at[e], p_ssem, p_rsem, partner)
     p_copy.start()
@@ -213,6 +249,7 @@
         wanted = (line + level[t] * crow).astype(jnp.float32)
         pick[t] = (jnp.abs(rows - wanted) < 0.5).astype(jnp.bfloat16)
 
+    round_on(0)
     jac_load.wait()
     if rem:
         tail[...] = jnp.zeros_like(tail)
@@ -223,18 +260,17 @@
             return tail[at]
         return jac_v[at, :, :, c * 128 : (c + 1) * 128]
 
-    def observe(t):
-        def measure(base, carry):
-            for u in range(4):
-                j = base * 4 + u
-                row = lax.rem(rows_s[0, j], crow)
-                total = jnp.zeros((slots // 8, 8, 128), jnp.float32)
-                for c in range(tiles):
-                    total = total + strip(j, c) * lines[row, :, c * 128 : (c + 1) * 128]
-                part_v[j] = total
-            return carry
-
-        lax.fori_loop(0, blocks // 4, measure, 0)
+    def measure(t):
+        def one(j):
+            row = lax.rem(rows_s[0, j], crow)
+            total = strip(j, 0) * lines[t, row, :, spans[0]]
+            for c in range(1, tiles):
+                total = total + strip(j, c) * lines[t, row, :, spans[c]]
+            part_v[j] = total
+
+        return [functools.partial(one, j) for j in range(blocks)]
+
+    def place(t):
         evolved = jnp.sum(part_v[...], axis=-1, keepdims=True)
         wgt[...] = prc_b[...] * (evolved - val_b[...])
         for c in range(0, tiles, 2):
@@ -245,15 +281,53 @@
             hi, lo = split(jnp.concatenate(pieces, axis=1))
             adj[t, 0:crow, c * 128 : c * 128 + hi.shape[1]] = mm(pick[t], hi, NN) + mm(pick[t], lo, NN)
 
-    def back(t):
-        g = adj[t]
-        return (
-            coef[t, 0] * g
-            + turn(coef[t, 1] * g, 1, 1)
-            + turn(coef[t, 2] * g, -1, 1)
-            + turn(coef[t, 3] * g, 1, 0)
-            + turn(coef[t, 4] * g, -1, 0)
-        )
+    def beside(tasks, done, of):
+        for task in tasks[len(tasks) * done // of : len(tasks) * (done + 1) // of]:
+            task()
+
+    lane = lax.broadcasted_iota(jnp.int32, (24, 128), 1)
+    starts, stops = lane == 0, lane == 127
+    spans = [slice(c * 128, (c + 1) * 128) for c in range(tiles)]
+
+    def forward(t, src, emit):
+        east = turn(src[:, spans[-1]], 1, 1)
+        here = src[:, spans[0]]
+        west = first_west = turn(here, -1, 1)
+        for c in range(tiles):
+            f, f_west, f_east = here, west, turn(here, 1, 1)
+            if c + 1 < tiles:
+                here = src[:, spans[c + 1]]
+                west = turn(here, -1, 1)
+            after = west if c + 1 < tiles else first_west
+            emit(c, (
+                coef[t, 0, :, spans[c]] * f
+                + coef[t, 1, :, spans[c]] * jnp.where(stops, after, f_west)
+                + coef[t, 2, :, spans[c]] * jnp.where(starts, east, f_east)
+                + coef[t, 3, :, spans[c]] * turn(f, -1, 0)
+                + coef[t, 4, :, spans[c]] * turn(f, 1, 0)
+            ))
+            east = f_east
+
+    def back(t, src, emit):
+        def moved(c):
+            g = src[:, spans[c]]
+            return g, turn(coef[t, 1, :, spans[c]] * g, 1, 1), turn(coef[t, 2, :, spans[c]] * g, -1, 1)
+
+        east = moved(tiles - 1)[1]
+        now = first = moved(0)
+        for c in range(tiles):
+            g, g_east, g_west = now
+            if c + 1 < tiles:
+                now = moved(c + 1)
+            after = now[2] if c + 1 < tiles else first[2]
+            emit(c, (
+                coef[t, 0, :, spans[c]] * g
+                + jnp.where(starts, east, g_east)
+                + jnp.where(stops, after, g_west)
+                + turn(coef[t, 3, :, spans[c]] * g, 1, 0)
+                + turn(coef[t, 4, :, spans[c]] * g, -1, 0)
+            ))
+            east = g_east
 
     def owner_copy(t, h):
         return remote(forc.at[t * E + h], rs_v.at[k], rs_ssem, rs_rsem, {"tm": level[t], "ens": h})
@@ -264,7 +338,9 @@
     edge_up = [edge_copy(t, 0, {"tm": level[t], "lat": lax.rem(b + 1, L), "ens": 0}) for t in range(half)]
     edge_down = [edge_copy(t, 1, {"tm": level[t], "lat": lax.rem(b + L - 1, L), "ens": E - 1}) for t in range(half)]
 
-    for t in range(half):
+    pairs = [(wide.at[0, t], adj.at[t]) for t in range(half)]
+
+    def advance(t, tasks):
         @pl.when(has_down)
         def _():
             h_up[t].wait_recv()
@@ -283,38 +359,66 @@
             wide[at, t, crow + 5 : crow + 6] = h_before[t, 4, at - 1 : at]
             wide[at, t, crow + 6 : crow + 8] = h_before[t, 1 + at]
         weigh(t, slice(crow, crow + 8))
-        for _ in range(STEPS):
-            f = wide[0, t]
-            wide[0, t] = (
-                coef[t, 0] * f
-                + coef[t, 1] * turn(f, -1, 1)
-                + coef[t, 2] * turn(f, 1, 1)
-                + coef[t, 3] * turn(f, -1, 0)
-                + coef[t, 4] * turn(f, 1, 0)
-            )
-        end_v[t] = wide[0, t, 0:crow]
-        for r in range(crow):
-            lines[r] = wide[0, t, r : r + 1]
-        observe(t)
-        @pl.when(has_later)
-        def _():
-            n_copy[t].wait_recv()
-
+        for at in range(STEPS):
+            src, dst = pairs[t][at % 2], pairs[t][(at + 1) % 2]
+
+            def emit(c, value):
+                if at + 1 < STEPS:
+                    dst[:, spans[c]] = value
+                else:
+                    end_v[t, :, spans[c]] = value[0:crow]
+                    for r in range(crow):
+                        lines[t, r, :, spans[c]] = value[r : r + 1]
+                beside(tasks, at * tiles + c, STEPS * tiles)
+
+            forward(t, src, emit)
+
+    def retreat(t, tasks):
         scale = jnp.where(has_later, mp_ref[level[t]], 0.0)
         adj[t, 0:crow, 0:lon] = adj[t, 0:crow, 0:lon] - scale * (nxt_v[t] - end_v[t, :, 0:lon])
         extend(adj, (t,), lon)
         adj[t, crow : crow + 8] = jnp.zeros((8, width), jnp.float32)
-        for h in range(E):
-            forc[t * E + h] = adj[t, h * 8 : h * 8 + 8]
-        rim = jnp.zeros((8, width), jnp.float32)
-        for _ in range(STEPS - 1):
-            adj[t] = back(t)
-            for h in range(E):
-                forc[t * E + h] += adj[t, h * 8 : h * 8 + 8]
-            rim = rim + adj[t, crow : crow + 8]
-        edge[0, t] = rim[0:4]
-        edge[1, t] = rim[4:8]
-
+        for at in range(STEPS - 1):
+            src, dst = pairs[t][(at + 1) % 2], pairs[t][at % 2]
+
+            def emit(c, value):
+                dst[:, spans[c]] = value
+                for h in range(E):
+                    rows = slice(h * 8, h * 8 + 8)
+                    base = adj[t, rows, spans[c]] if at == 0 else forc[t * E + h, :, spans[c]]
+                    forc[t * E + h, :, spans[c]] = base + value[rows]
+                rim = value[crow:] if at == 0 else rims[:, spans[c]] + value[crow:]
+                if at < STEPS - 2:
+                    rims[:, spans[c]] = rim
+                else:
+                    edge[0, t, :, spans[c]] = rim[0:4]
+                    edge[1, t, :, spans[c]] = rim[4:8]
+                beside(tasks, at * tiles + c, (STEPS - 1) * tiles)
+
+            back(t, src, emit)
+
+    round_on(1)
+    advance(0, [])
+    for t in range(half):
+        if t < half // 2:
+            @pl.when(has_later)
+            def _():
+                e_copy(t).start()
+
+        first_tasks = measure(t) if t == 0 else []
+        if t + 1 < half:
+            advance(t + 1, first_tasks)
+        else:
+            for task in first_tasks:
+                task()
+        place(t)
+        @pl.when(has_later)
+        def _():
+            n_copy[t].wait_recv()
+
+        retreat(t, measure(t + 1) if t + 1 < half else [])
+        if t == 0:
+            round_on(2)
         @pl.when(has_up)
         def _():
             edge_up[t].start()
@@ -334,10 +438,32 @@
             def _():
                 owner_copy(t, h).start()
 
+    owner = lax.rem(k + E * half - k // E, E) == e
+
+    def all_but(ref, some):
+        return ref.at[pl.ds(0, ref.shape[0] - some)]
+
+    def sent_all():
+        for some, when in ((1, owner), (0, jnp.logical_not(owner))):
+            @pl.when(when)
+            def _():
+                remote(all_but(forc, some), all_but(forc, some), rs_ssem, rs_rsem, partner).wait_send()
+
+    def send_end():
+        for t in range(half // 2, half):
+            e_copy(t).start()
+
+    @pl.when(has_later & (k != 1))
+    def _():
+        send_end()
+
     for t in range(half):
-        adj[t] = back(t)
-        a_up_v[t] = adj[t, crow : crow + 4]
-        a_down_v[t] = adj[t, crow + 4 : crow + 8]
+        def emit(c, value):
+            last[t, :, spans[c]] = value[0:crow]
+            a_up_v[t, :, spans[c]] = value[crow : crow + 4]
+            a_down_v[t, :, spans[c]] = value[crow + 4 :]
+
+        back(t, (adj.at[t], wide.at[0, t])[STEPS % 2 == 0], emit)
     a_up = remote(a_up_v, a_before, a_ssem.at[0], a_rsem.at[0], up)
     a_down = remote(a_down_v, a_after, a_ssem.at[1], a_rsem.at[1], down)
 
@@ -349,20 +475,21 @@
     def _():
         a_down.start()
 
-    owner = k // half == e
-
-    def all_but(ref, some):
-        return ref.at[pl.ds(0, ref.shape[0] - some)]
-
-    for some, when in ((1, owner), (0, jnp.logical_not(owner))):
-        @pl.when(when)
-        def _():
-            remote(all_but(forc, some), all_but(forc, some), rs_ssem, rs_rsem, partner).wait_send()
-
-    @pl.when(has_later)
-    def _():
-        for t in range(half):
-            e_copy(t).start()
+    @pl.when(k == 1)
+    def _():
+        sent_all()
+
+        @pl.when(e == 0)
+        def _():
+            pl.semaphore_signal(pair_sem, inc=1, device_id=partner, device_id_type=MESH)
+
+        @pl.when(e != 0)
+        def _():
+            pl.semaphore_wait(pair_sem, 1)
+
+        @pl.when(has_later)
+        def _():
+            send_end()
 
     p_copy.wait_recv()
     for some, when in ((1, owner), (0, jnp.logical_not(owner))):
@@ -390,21 +517,28 @@
     part = jnp.sum(part, axis=0, keepdims=True)
     ca_send[...] = part
     if direct:
-        crowd = [(dt, db, de) for dt in range(T) for db in range(L) for de in range(E) if dt or db or de]
-        pl.semaphore_wait(all_sem, L - 1)
+        crowd = [(dt, lat, de) for lat in range(L) for dt in range(T) for de in range(E)]
+        if not near:
+            pl.semaphore_wait(all_sem, L - 1)
     else:
-        crowd = [(dt, 0, de) for dt, de in group]
-
-    def seat(dt, db, de):
-        at, lat, ens = lax.rem(k + dt, T), lax.rem(b + db, L), lax.rem(e + de, E)
+        crowd = [(dt, b, de) for dt, de in group]
+
+    def seat(dt, lat, de):
+        at, ens = lax.rem(k + dt, T), lax.rem(e + de, E)
         index = (at * L + lat) * E + ens if direct else at * E + ens
         return index, {"tm": at, "lat": lat, "ens": ens}
 
     sums = cb_v if direct else ca_v
-    me, _ = seat(0, 0, 0)
+    me, _ = seat(0, b, 0)
     sums[me] = part
-    for dt, db, de in crowd:
-        remote(ca_send, sums.at[me], ca_ssem, ca_rsem, seat(dt, db, de)[1]).start()
+    for dt, lat, de in crowd:
+        copy = remote(ca_send, sums.at[me], ca_ssem, ca_rsem, seat(dt, lat, de)[1])
+        if dt or de:
+            copy.start()
+        else:
+            @pl.when(lat != b)
+            def _():
+                copy.start()
 
     @pl.when(has_prior)
     def _():
@@ -422,11 +556,12 @@
     for t in range(half):
         prec = mp_ref[level[t]]
         gap = jnp.zeros((crow - 8, lon), jnp.float32)
-        rims = jnp.concatenate([a_before[t][:, 0:lon], gap, a_after[t][:, 0:lon]], axis=0)
-        grad_v[level[t]] = adj[t, 0:crow, 0:lon] + rims + prec * (fields[0, t] - prior_v[t, :, 0:lon])
-    g_copy = remote(grad_v.at[own], grad_v.at[own], g_ssem, g_rsem, partner)
-    g_copy.start()
-    others = sums.at[pl.ds(0, len(crowd))]
+        rims_in = jnp.concatenate([a_before[t][:, 0:lon], gap, a_after[t][:, 0:lon]], axis=0)
+        grad_v[level[t]] = last[t, :, 0:lon] + rims_in + prec * (fields[0, t] - prior_v[t, :, 0:lon])
+        remote(grad_v.at[level[t]], grad_v.at[level[t]], g_ssem, g_rsem, partner).start()
+    grad_half = grad_v.at[pl.ds(0, half)]
+    g_copy = remote(grad_half, grad_half, g_ssem, g_rsem, partner)
+    others = all_but(sums, 1)
     remote(others, others, ca_ssem, ca_rsem, partner).wait_recv()
     if not direct:
         part = ca_v[0]
@@ -439,6 +574,10 @@
         bands = remote(all_but(cb_v, 1), all_but(cb_v, 1), cb_ssem, cb_rsem, partner)
         bands.wait_recv()
     g_copy.wait_recv()
+
+    @pl.when(k != 1)
+    def _():
+        sent_all()
 
     @pl.when(has_up)
     def _():
@@ -518,11 +657,12 @@
             buf(3, half, 24, width), buf(half, 5, 24, width), buf(half, 24, width),
             buf(half, 5, 2, width), buf(half, 5, 2, width), buf(half, 5, 2, width), buf(half, 5, 2, width),
             buf(half, 4, width), buf(half, 4, width), buf(half, 4, width), buf(half, 4, width),
-            buf(half, crow, width), buf(crow, 1, width), buf(half, crow, lon), buf(half, crow, width),
+            buf(half, crow, width), buf(half, crow, 1, width), buf(half, crow, width), buf(8, width), buf(half, crow, lon), buf(half, crow, width),
             buf(half * E, 8, width), buf(2, half, 4, width), buf(T, 8, width), buf(T, 4, width),
             buf(1, 128), buf(T * E, 1, 128), buf(1, 128),
             dma((3,)), dma((6,)), dma((2,)), dma((2, half)), dma((2,)), dma((2,)), dma, dma((half,)), dma, dma((half,)),
             dma, dma, dma, dma, dma((2,)), dma, dma, dma, dma, dma, dma, dma, pltpu.SemaphoreType.REGULAR,
+            pltpu.SemaphoreType.REGULAR((3,)), pltpu.SemaphoreType.REGULAR,
         ],
         compiler_params=pltpu.CompilerParams(
             collective_id=0, has_side_effects=True, vmem_limit_bytes=56 * 1024 * 1024

time: 24.2 us -> 23.2 us (0.959)
  Pallas kernels: 23.4 us -> 22.4 us
    pallas_call x1, Pallas kernels: 22.4 us -> 21.4 us  [on_device(): pl.pallas_call(functools.partial(kernel, T, L, E), out_shape=(buf(levels,...]
where the time goes in v2:
time: 23.2 us; the launch traced here: 23 us
  Pallas kernels  22.4 us (97%)
  between operations  0.64 us (3%)
    pallas_call x1, Pallas kernels, on_device(): pl.pallas_call(functools.partial(kernel, T, L, E), out_shape=(buf(levels,...  21.4 us
    pallas_call x1, Pallas kernels, on_device(): pl.pallas_call(finish, out_shape=(jax.ShapeDtypeStruct((levels, crow, lon...  0.97 us

profile of v2, /device:TPU:0, one launch (start us, length us, event | category | flops | bytes accessed | tf_op | source)
XLA Modules:
  0.0 23.0 jit_solution(13735339673272185237)
XLA Ops:
  0.6 21.4 %shard_map.113 = (f32[4,16,1440]{2,1,0:T(8,128)S(1)}, f32[2,16,2,8,1440]{4,3,2,1,0:T(8,128)S(1)}, f32[32,1,128]{2,1,0:T(1,128)S(1)}) custom-call(s32[1,32]{1,0:T(1,128)} %rows_hbm.1, s32[1,32]{1,0:T(1,128)} %cnt_hbm.1, f32[16,32]{1,0:T(8,128)} %bitcast.18, f32[16,32]{1,0:T(8,128)} %bitcast.19, f32[4]{0:T(128)} %mp_hbm.1, f32[4,16,1440]{2,1,0:T(8,128)} %bitcast.15, ...), custom_call_target="tpu_custom_call" | custom-call | tf_op jit(solution)/shard_map/pallas_call | solution.py:643
  22.0 1.0 %shard_map.114 = (f32[4,16,1440]{2,1,0:T(8,128)}, f32[16,1440]{1,0:T(8,128)}) custom-call(f32[4,16,1440]{2,1,0:T(8,128)S(1)} %get-tuple-element.7.grad_v, f32[2,16,2,8,1440]{4,3,2,1,0:T(8,128)S(1)} %get-tuple-element.8.pert_v, f32[32,1,128]{2,1,0:T(1,128)S(1)} %get-tuple-element.9.cb_v), custom_call_target="tpu_custom_call" | custom-call | tf_op jit(solution)/shard_map/pallas_call | solution.py:676

commit v3 on v2

--- a/solution.py
+++ b/solution.py
@@ -247,7 +247,7 @@
     line = lax.broadcasted_iota(jnp.int32, (crow, blocks * 8), 0)
     for t in range(half):
         wanted = (line + level[t] * crow).astype(jnp.float32)
-        pick[t] = (jnp.abs(rows - wanted) < 0.5).astype(jnp.bfloat16)
+        pick[t * crow : (t + 1) * crow] = (jnp.abs(rows - wanted) < 0.5).astype(jnp.bfloat16)
 
     round_on(0)
     jac_load.wait()
@@ -260,17 +260,20 @@
             return tail[at]
         return jac_v[at, :, :, c * 128 : (c + 1) * 128]
 
-    def measure(t):
-        def one(j):
-            row = lax.rem(rows_s[0, j], crow)
-            total = strip(j, 0) * lines[t, row, :, spans[0]]
-            for c in range(1, tiles):
-                total = total + strip(j, c) * lines[t, row, :, spans[c]]
-            part_v[j] = total
-
-        return [functools.partial(one, j) for j in range(blocks)]
-
-    def place(t):
+    def observe():
+        def measure(base, carry):
+            for u in range(8):
+                j = base * 8 + u
+                row = rows_s[0, j]
+                slot = lax.rem(row // (crow * E) + half - shift(k), half)
+                row = lax.rem(row, crow)
+                total = strip(j, 0) * lines[slot, row, :, spans[0]]
+                for c in range(1, tiles):
+                    total = total + strip(j, c) * lines[slot, row, :, spans[c]]
+                part_v[j] = total
+            return carry
+
+        lax.fori_loop(0, blocks // 8, measure, 0)
         evolved = jnp.sum(part_v[...], axis=-1, keepdims=True)
         wgt[...] = prc_b[...] * (evolved - val_b[...])
         for c in range(0, tiles, 2):
@@ -279,11 +282,9 @@
                 piece = jnp.sum(strip(slice(None), cc) * wgt[...], axis=1)
                 pieces.append(piece.reshape(blocks * 8, 128))
             hi, lo = split(jnp.concatenate(pieces, axis=1))
-            adj[t, 0:crow, c * 128 : c * 128 + hi.shape[1]] = mm(pick[t], hi, NN) + mm(pick[t], lo, NN)
-
-    def beside(tasks, done, of):
-        for task in tasks[len(tasks) * done // of : len(tasks) * (done + 1) // of]:
-            task()
+            placed = mm(pick[...], hi, NN) + mm(pick[...], lo, NN)
+            for t in range(half):
+                adj[t, 0:crow, c * 128 : c * 128 + hi.shape[1]] = placed[t * crow : (t + 1) * crow]
 
     lane = lax.broadcasted_iota(jnp.int32, (24, 128), 1)
     starts, stops = lane == 0, lane == 127
@@ -340,7 +341,7 @@
 
     pairs = [(wide.at[0, t], adj.at[t]) for t in range(half)]
 
-    def advance(t, tasks):
+    def advance(t):
         @pl.when(has_down)
         def _():
             h_up[t].wait_recv()
@@ -369,11 +370,10 @@
                     end_v[t, :, spans[c]] = value[0:crow]
                     for r in range(crow):
                         lines[t, r, :, spans[c]] = value[r : r + 1]
-                beside(tasks, at * tiles + c, STEPS * tiles)
 
             forward(t, src, emit)
 
-    def retreat(t, tasks):
+    def retreat(t):
         scale = jnp.where(has_later, mp_ref[level[t]], 0.0)
         adj[t, 0:crow, 0:lon] = adj[t, 0:crow, 0:lon] - scale * (nxt_v[t] - end_v[t, :, 0:lon])
         extend(adj, (t,), lon)
@@ -391,32 +391,27 @@
                 if at < STEPS - 2:
                     rims[:, spans[c]] = rim
                 else:
-                    edge[0, t, :, spans[c]] = rim[0:4]
-                    edge[1, t, :, spans[c]] = rim[4:8]
-                beside(tasks, at * tiles + c, (STEPS - 1) * tiles)
+                    for r in range(3):
+                        edge[0, t, r, :, spans[c]] = rim[r : r + 1]
+                        edge[1, t, r, :, spans[c]] = rim[r + 5 : r + 6]
 
             back(t, src, emit)
 
     round_on(1)
-    advance(0, [])
     for t in range(half):
+        advance(t)
         if t < half // 2:
             @pl.when(has_later)
             def _():
                 e_copy(t).start()
 
-        first_tasks = measure(t) if t == 0 else []
-        if t + 1 < half:
-            advance(t + 1, first_tasks)
-        else:
-            for task in first_tasks:
-                task()
-        place(t)
+    observe()
+    for t in range(half):
         @pl.when(has_later)
         def _():
             n_copy[t].wait_recv()
 
-        retreat(t, measure(t + 1) if t + 1 < half else [])
+        retreat(t)
         if t == 0:
             round_on(2)
         @pl.when(has_up)
@@ -501,13 +496,14 @@
     def _():
         remote(edge_v, edge_v, ed_ssem.at[0], ed_rsem, partner).wait_recv()
 
-    total, rim = rs_v[0], edge_v[0]
+    total = rs_v[0]
     for at in range(1, T):
         total = total + rs_v[at]
-        rim = rim + edge_v[at]
-    line = lax.broadcasted_iota(jnp.int32, (8, width), 0)
-    rim = jnp.concatenate([rim, rim], axis=0)
-    total = total + jnp.where((line < 4) == (e == 0), rim, 0.0)
+    inner = [sum((edge_v[at, r] for at in range(1, T)), edge_v[0, r]) for r in range(3)]
+    blank = jnp.zeros((5, width), jnp.float32)
+    total = total + jnp.where(
+        e == 0, jnp.concatenate(inner + [blank], axis=0), jnp.concatenate([blank] + inner, axis=0)
+    )
     total = total[:, 0:lon]
     lane = lax.broadcasted_iota(jnp.int32, (8, 128), 1)
     part = jnp.zeros((8, 128), jnp.float32)
@@ -653,12 +649,12 @@
             pltpu.SMEM((1, blocks), jnp.int32), pltpu.VMEM((1, blocks), jnp.int32), pltpu.VMEM((1, blocks), jnp.int32),
             buf(slots, blocks), buf(slots, blocks), pltpu.SMEM((levels,), f32),
             buf(3, half, crow, lon), buf(blocks, slots // 8, 8, lon), table, table, table, table, table,
-            buf(half, crow, blocks * 8, kind=jnp.bfloat16),
+            buf(half * crow, blocks * 8, kind=jnp.bfloat16),
             buf(3, half, 24, width), buf(half, 5, 24, width), buf(half, 24, width),
             buf(half, 5, 2, width), buf(half, 5, 2, width), buf(half, 5, 2, width), buf(half, 5, 2, width),
             buf(half, 4, width), buf(half, 4, width), buf(half, 4, width), buf(half, 4, width),
             buf(half, crow, width), buf(half, crow, 1, width), buf(half, crow, width), buf(8, width), buf(half, crow, lon), buf(half, crow, width),
-            buf(half * E, 8, width), buf(2, half, 4, width), buf(T, 8, width), buf(T, 4, width),
+            buf(half * E, 8, width), buf(2, half, 3, 1, width), buf(T, 8, width), buf(T, 3, 1, width),
             buf(1, 128), buf(T * E, 1, 128), buf(1, 128),
             dma((3,)), dma((6,)), dma((2,)), dma((2, half)), dma((2,)), dma((2,)), dma, dma((half,)), dma, dma((half,)),
             dma, dma, dma, dma, dma((2,)), dma, dma, dma, dma, dma, dma, dma, pltpu.SemaphoreType.REGULAR,

time: 23.2 us -> 22.8 us (0.983)
  Pallas kernels: 22.4 us -> 22 us
    pallas_call x1, Pallas kernels: 21.4 us -> 21 us  [on_device(): pl.pallas_call(functools.partial(kernel, T, L, E), out_shape=(buf(levels,...]
where the time goes in v3:
time: 22.8 us; the launch traced here: 22.6 us
  Pallas kernels  22 us (96%)
  between operations  0.64 us (3%)
    pallas_call x1, Pallas kernels, on_device(): pl.pallas_call(functools.partial(kernel, T, L, E), out_shape=(buf(levels,...  21 us
    pallas_call x1, Pallas kernels, on_device(): pl.pallas_call(finish, out_shape=(jax.ShapeDtypeStruct((levels, crow, lon...  0.97 us

profile of v3, /device:TPU:0, one launch (start us, length us, event | category | flops | bytes accessed | tf_op | source)
XLA Modules:
  0.0 22.6 jit_solution(12346665092393268868)
XLA Ops:
  0.6 21.0 %shard_map.113 = (f32[4,16,1440]{2,1,0:T(8,128)S(1)}, f32[2,16,2,8,1440]{4,3,2,1,0:T(8,128)S(1)}, f32[32,1,128]{2,1,0:T(1,128)S(1)}) custom-call(s32[1,32]{1,0:T(1,128)} %rows_hbm.1, s32[1,32]{1,0:T(1,128)} %cnt_hbm.1, f32[16,32]{1,0:T(8,128)} %bitcast.18, f32[16,32]{1,0:T(8,128)} %bitcast.19, f32[4]{0:T(128)} %mp_hbm.1, f32[4,16,1440]{2,1,0:T(8,128)} %bitcast.15, ...), custom_call_target="tpu_custom_call" | custom-call | tf_op jit(solution)/shard_map/pallas_call | solution.py:639
  21.7 1.0 %shard_map.114 = (f32[4,16,1440]{2,1,0:T(8,128)}, f32[16,1440]{1,0:T(8,128)}) custom-call(f32[4,16,1440]{2,1,0:T(8,128)S(1)} %get-tuple-element.7.grad_v, f32[2,16,2,8,1440]{4,3,2,1,0:T(8,128)S(1)} %get-tuple-element.8.pert_v, f32[32,1,128]{2,1,0:T(1,128)S(1)} %get-tuple-element.9.cb_v), custom_call_target="tpu_custom_call" | custom-call | tf_op jit(solution)/shard_map/pallas_call | solution.py:672

commit v4 on v3

--- a/solution.py
+++ b/solution.py
@@ -43,28 +43,35 @@
     T, L, E,
     rows_hbm, cnt_hbm, val_hbm, prc_hbm, mp_hbm, inc_hbm, wlon_hbm, wlat_hbm, jac_hbm, pert_hbm,
     grad_v, pert_v, cb_v,
-    rows_s, rows_ref, cnt_ref, val_ref, prc_ref, mp_ref, fields, jac_v, tail, val_b, prc_b, part_v, wgt, pick,
+    rows_s, whole_ref, slot_ref, mp_ref, fields, jac_v, tail, val_b, prc_b, part_v, wgt, pick,
     wide, coef, adj, h_first, h_last, h_after, h_before, a_up_v, a_down_v, a_after, a_before,
     end_v, lines, last, rims, nxt_v, prior_v, forc, edge, rs_v, edge_v, ca_send, ca_v, cb_send,
     load_sem, small_sem, h_ssem, h_rsem, a_ssem, a_rsem, t_ssem, t_rsem, e_ssem, e_rsem, p_ssem, p_rsem,
-    rs_ssem, rs_rsem, ed_ssem, ed_rsem, ca_ssem, ca_rsem, cb_ssem, cb_rsem, g_ssem, g_rsem, all_sem, round_sem, pair_sem,
+    rs_ssem, rs_rsem, ed_ssem, ed_rsem, ca_ssem, ca_rsem, cb_ssem, cb_rsem, g_rsem, all_sem, round_sem,
 ):
     k, b, e = lax.axis_index("tm"), lax.axis_index("lat"), lax.axis_index("ens")
     _, half, crow, lon = fields.shape
     width = wide.shape[-1]
     members = pert_v.shape[1]
-    slots, blocks = val_ref.shape
+    _, slots, blocks = slot_ref.shape
     tiles, rem = width // 128, lon % 128
     other = 1 - e
 
-    def shift(at):
-        return lax.rem(at + e + 1, half)
-
-    def spot(t, at, there):
-        return lax.rem(t + shift(at) + half - shift(there), half)
-
-    order = [lax.rem(shift(k) + t, half) for t in range(half)]
-    level = [at * E + lax.rem(e + at, E) for at in order]
+    direct = T * L * E <= 64
+    near = direct and T == 4 and E == 2
+    role = lax.rem(e + k // 2, 2) if near else e
+
+    def shift(at, core):
+        return lax.rem(at + 1 + core, half)
+
+    def keeper(at):
+        return lax.rem(e + k // 2 + at // 2, 2) if near else e
+
+    def spot(t, at, core, there, other_core):
+        return lax.rem(t + shift(at, core) + half - shift(there, other_core), half)
+
+    order = [lax.rem(shift(k, e) + t, half) for t in range(half)]
+    level = [role * half + at for at in order]
 
     def local(src, dst, sem):
         return pltpu.make_async_copy(src, dst, sem)
@@ -74,21 +81,19 @@
             local(ref.at[level[t]], fields.at[at, t], load_sem.at[0]).start()
     small = [
         local(rows_hbm, rows_s, small_sem.at[0]),
-        local(rows_hbm, rows_ref, small_sem.at[1]),
-        local(cnt_hbm, cnt_ref, small_sem.at[2]),
-        local(val_hbm, val_ref, small_sem.at[3]),
-        local(prc_hbm, prc_ref, small_sem.at[4]),
-        local(mp_hbm, mp_ref, small_sem.at[5]),
+        local(rows_hbm, whole_ref.at[0], small_sem.at[1]),
+        local(cnt_hbm, whole_ref.at[1], small_sem.at[1]),
+        local(val_hbm, slot_ref.at[0], small_sem.at[2]),
+        local(prc_hbm, slot_ref.at[1], small_sem.at[2]),
+        local(mp_hbm, mp_ref, small_sem.at[3]),
     ]
 
     barrier = pltpu.get_barrier_semaphore()
-    direct = T * L * E <= 64
     group = [(dt, de) for dt in range(T) for de in range(E) if dt or de]
 
     def mate(dt, de):
         return {"tm": lax.rem(k + dt, T), "ens": lax.rem(e + de, E)}
 
-    near = direct and T == 4 and E == 2
     ring = [
         ({"ens": 1 - e}, None),
         ({"tm": k + 1 - 2 * lax.rem(k, 2)}, None),
@@ -99,7 +104,7 @@
     middle = (k == 1) | (k == 2)
 
     def greet(sem, extra):
-        for device, when in ring + ([({"tm": T - 1 - k}, middle)] if extra else []):
+        for device, when in ring + ([({"tm": T - 1 - k, "ens": other}, middle)] if extra else []):
             if when is None:
                 pl.semaphore_signal(sem, inc=1, device_id=device, device_id_type=MESH)
             else:
@@ -113,9 +118,9 @@
 
     def round_on(at):
         if near:
-            meet(round_sem.at[at], False)
+            meet(round_sem.at[at % 2], False)
             if at < 2:
-                greet(round_sem.at[at + 1], False)
+                greet(round_sem.at[(at + 1) % 2], False)
 
     if near:
         greet(barrier, True)
@@ -138,8 +143,8 @@
     has_later, has_prior = k < T - 1, k > 0
 
     local(fields, fields, load_sem.at[0]).wait()
-    jac_load = local(jac_hbm, jac_v, load_sem.at[1])
-    pert_load = local(pert_hbm, pert_v.at[e], load_sem.at[2])
+    jac_load = local(jac_hbm, jac_v, load_sem.at[0])
+    pert_load = local(pert_hbm, pert_v.at[e], load_sem.at[1])
     for item in small + [pert_load, jac_load]:
         item.start()
     for t in range(half):
@@ -167,13 +172,13 @@
     h_up = [remote(h_last.at[t], h_before.at[t], h_ssem.at[0], h_rsem.at[0, t], up) for t in range(half)]
     h_down = [remote(h_first.at[t], h_after.at[t], h_ssem.at[1], h_rsem.at[1, t], down) for t in range(half)]
     n_copy = [
-        remote(fields.at[0, spot(t, prior_k, k)], nxt_v.at[t], t_ssem, t_rsem.at[t], {"tm": prior_k})
+        remote(fields.at[0, spot(t, prior_k, keeper(prior_k), k, e)], nxt_v.at[t], t_ssem, t_rsem.at[t], {"tm": prior_k, "ens": keeper(prior_k)})
         for t in range(half)
     ]
 
     def e_copy(t):
-        there = spot(t, k, later_k)
-        return remote(end_v.at[t], prior_v.at[there], e_ssem, e_rsem.at[there], {"tm": later_k})
+        there = spot(t, k, e, later_k, keeper(later_k))
+        return remote(end_v.at[t], prior_v.at[there], e_ssem, e_rsem, {"tm": later_k, "ens": keeper(later_k)})
 
     for t in range(half):
         @pl.when(has_up)
@@ -184,6 +189,7 @@
         def _():
             h_down[t].start()
 
+    for t in range(half):
         @pl.when(has_prior)
         def _():
             n_copy[t].start()
@@ -192,7 +198,6 @@
         greet(round_sem.at[0], False)
     pert_load.wait()
     p_copy = remote(pert_v.at[e], pert_v.at[e], p_ssem, p_rsem, partner)
-    p_copy.start()
 
     @pl.when(jnp.logical_not(has_up))
     def _():
@@ -232,18 +237,20 @@
         for at in (1, 2):
             wide[at, t, crow : crow + 8] = jnp.zeros((8, width), jnp.float32)
 
-    for item in small:
+    for item in (
+        small[0], small[-1], local(whole_ref, whole_ref, small_sem.at[1]), local(slot_ref, slot_ref, small_sem.at[2])
+    ):
         item.wait()
     deep = lax.broadcasted_iota(jnp.int32, (slots, blocks), 0)
-    precisions = jnp.where(deep < cnt_ref[...], prc_ref[...], 0.0)
-    values = val_ref[...]
+    precisions = jnp.where(deep < whole_ref[1], slot_ref[1], 0.0)
+    values = slot_ref[0]
     for j in range(blocks):
         prc_b[j] = jnp.broadcast_to(precisions[:, j : j + 1], (slots, 128)).reshape(slots // 8, 8, 128)
         val_b[j] = jnp.broadcast_to(values[:, j : j + 1], (slots, 128)).reshape(slots // 8, 8, 128)
     column = lax.broadcasted_iota(jnp.int32, (blocks, blocks * 8), 1)
     block = lax.broadcasted_iota(jnp.int32, (blocks, blocks * 8), 0)
     spread = ((column >= block * 8) & (column < (block + 1) * 8)).astype(jnp.float32)
-    rows = mm(jnp.broadcast_to(rows_ref[...].astype(jnp.float32), (8, blocks)), spread, NN, HIGHEST)[0:1]
+    rows = mm(jnp.broadcast_to(whole_ref[0].astype(jnp.float32), (8, blocks)), spread, NN, HIGHEST)[0:1]
     line = lax.broadcasted_iota(jnp.int32, (crow, blocks * 8), 0)
     for t in range(half):
         wanted = (line + level[t] * crow).astype(jnp.float32)
@@ -265,7 +272,7 @@
             for u in range(8):
                 j = base * 8 + u
                 row = rows_s[0, j]
-                slot = lax.rem(row // (crow * E) + half - shift(k), half)
+                slot = lax.rem(row // crow + half - shift(k, e), half)
                 row = lax.rem(row, crow)
                 total = strip(j, 0) * lines[slot, row, :, spans[0]]
                 for c in range(1, tiles):
@@ -397,9 +404,31 @@
 
             back(t, src, emit)
 
+    def send_set(t, turn_of):
+        @pl.when(has_up & turn_of)
+        def _():
+            edge_up[t].start()
+
+        @pl.when(has_down & turn_of)
+        def _():
+            edge_down[t].start()
+
+        for h in range(E):
+            here = (k == level[t]) & (e == h)
+
+            @pl.when(here & turn_of)
+            def _():
+                rs_v[k] = forc[t * E + h]
+
+            @pl.when(jnp.logical_not(here) & turn_of)
+            def _():
+                owner_copy(t, h).start()
+
     round_on(1)
     for t in range(half):
         advance(t)
+        if t == half - 1:
+            p_copy.start()
         if t < half // 2:
             @pl.when(has_later)
             def _():
@@ -414,26 +443,9 @@
         retreat(t)
         if t == 0:
             round_on(2)
-        @pl.when(has_up)
-        def _():
-            edge_up[t].start()
-
-        @pl.when(has_down)
-        def _():
-            edge_down[t].start()
-
-        for h in range(E):
-            here = (k == level[t]) & (e == h)
-
-            @pl.when(here)
-            def _():
-                rs_v[k] = forc[t * E + h]
-
-            @pl.when(jnp.logical_not(here))
-            def _():
-                owner_copy(t, h).start()
-
-    owner = lax.rem(k + E * half - k // E, E) == e
+        send_set(t, e == 0 if near and t == half - 1 else e >= 0)
+
+    owner = k // half == role
 
     def all_but(ref, some):
         return ref.at[pl.ds(0, ref.shape[0] - some)]
@@ -448,10 +460,6 @@
         for t in range(half // 2, half):
             e_copy(t).start()
 
-    @pl.when(has_later & (k != 1))
-    def _():
-        send_end()
-
     for t in range(half):
         def emit(c, value):
             last[t, :, spans[c]] = value[0:crow]
@@ -459,6 +467,13 @@
             a_down_v[t, :, spans[c]] = value[crow + 4 :]
 
         back(t, (adj.at[t], wide.at[0, t])[STEPS % 2 == 0], emit)
+    if near:
+        send_set(half - 1, e != 0)
+
+    @pl.when(has_later & (k != 1))
+    def _():
+        send_end()
+
     a_up = remote(a_up_v, a_before, a_ssem.at[0], a_rsem.at[0], up)
     a_down = remote(a_down_v, a_after, a_ssem.at[1], a_rsem.at[1], down)
 
@@ -476,11 +491,11 @@
 
         @pl.when(e == 0)
         def _():
-            pl.semaphore_signal(pair_sem, inc=1, device_id=partner, device_id_type=MESH)
+            pl.semaphore_signal(round_sem.at[1], inc=1, device_id=partner, device_id_type=MESH)
 
         @pl.when(e != 0)
         def _():
-            pl.semaphore_wait(pair_sem, 1)
+            pl.semaphore_wait(round_sem.at[1], 1)
 
         @pl.when(has_later)
         def _():
@@ -538,8 +553,7 @@
 
     @pl.when(has_prior)
     def _():
-        for t in range(half):
-            remote(end_v.at[t], prior_v.at[t], e_ssem, e_rsem.at[t], partner).wait_recv()
+        remote(end_v, prior_v, e_ssem, e_rsem, partner).wait_recv()
 
     @pl.when(has_down)
     def _():
@@ -549,14 +563,15 @@
     def _():
         a_down.wait_recv()
 
+    p_copy.wait_send()
     for t in range(half):
         prec = mp_ref[level[t]]
         gap = jnp.zeros((crow - 8, lon), jnp.float32)
         rims_in = jnp.concatenate([a_before[t][:, 0:lon], gap, a_after[t][:, 0:lon]], axis=0)
         grad_v[level[t]] = last[t, :, 0:lon] + rims_in + prec * (fields[0, t] - prior_v[t, :, 0:lon])
-        remote(grad_v.at[level[t]], grad_v.at[level[t]], g_ssem, g_rsem, partner).start()
+        remote(grad_v.at[level[t]], grad_v.at[level[t]], p_ssem, g_rsem, partner).start()
     grad_half = grad_v.at[pl.ds(0, half)]
-    g_copy = remote(grad_half, grad_half, g_ssem, g_rsem, partner)
+    g_copy = remote(grad_half, grad_half, p_ssem, g_rsem, partner)
     others = all_but(sums, 1)
     remote(others, others, ca_ssem, ca_rsem, partner).wait_recv()
     if not direct:
@@ -593,9 +608,8 @@
 
     @pl.when(has_later)
     def _():
-        remote(end_v, end_v, e_ssem, e_rsem.at[0], partner).wait_send()
-
-    p_copy.wait_send()
+        remote(end_v, end_v, e_ssem, e_rsem, partner).wait_send()
+
     g_copy.wait_send()
     remote(others, others, ca_ssem, ca_rsem, partner).wait_send()
     if not direct:
@@ -607,9 +621,10 @@
     g_out.start()
     ens, members, rows, _, lon = pert_v.shape
     count = ens * members
-    part = cb_v[0]
-    for at in range(1, cb_v.shape[0]):
-        part = part + cb_v[at]
+    parts = [cb_v[at] for at in range(cb_v.shape[0])]
+    while len(parts) > 1:
+        parts = [sum(parts[at + 1 : at + 2], parts[at]) for at in range(0, len(parts), 2)]
+    part = parts[0]
     factor = jnp.broadcast_to(part, (8, 128)) * (-1.0 / (count - 1.0))
     for h in range(rows):
         mixed = jnp.zeros((8, lon), jnp.float32)
@@ -646,8 +661,7 @@
         in_specs=[pl.BlockSpec(memory_space=pltpu.HBM)] * 10,
         out_specs=(vmem, vmem, vmem),
         scratch_shapes=[
-            pltpu.SMEM((1, blocks), jnp.int32), pltpu.VMEM((1, blocks), jnp.int32), pltpu.VMEM((1, blocks), jnp.int32),
-            buf(slots, blocks), buf(slots, blocks), pltpu.SMEM((levels,), f32),
+            pltpu.SMEM((1, blocks), jnp.int32), pltpu.VMEM((2, 1, blocks), jnp.int32), buf(2, slots, blocks), pltpu.SMEM((levels,), f32),
             buf(3, half, crow, lon), buf(blocks, slots // 8, 8, lon), table, table, table, table, table,
             buf(half * crow, blocks * 8, kind=jnp.bfloat16),
             buf(3, half, 24, width), buf(half, 5, 24, width), buf(half, 24, width),
@@ -656,9 +670,9 @@
             buf(half, crow, width), buf(half, crow, 1, width), buf(half, crow, width), buf(8, width), buf(half, crow, lon), buf(half, crow, width),
             buf(half * E, 8, width), buf(2, half, 3, 1, width), buf(T, 8, width), buf(T, 3, 1, width),
             buf(1, 128), buf(T * E, 1, 128), buf(1, 128),
-            dma((3,)), dma((6,)), dma((2,)), dma((2, half)), dma((2,)), dma((2,)), dma, dma((half,)), dma, dma((half,)),
-            dma, dma, dma, dma, dma((2,)), dma, dma, dma, dma, dma, dma, dma, pltpu.SemaphoreType.REGULAR,
-            pltpu.SemaphoreType.REGULAR((3,)), pltpu.SemaphoreType.REGULAR,
+            dma((2,)), dma((4,)), dma((2,)), dma((2, half)), dma((2,)), dma((2,)), dma, dma((half,)), dma, dma,
+            dma, dma, dma, dma, dma((2,)), dma, dma, dma, dma, dma, dma, pltpu.SemaphoreType.REGULAR,
+            pltpu.SemaphoreType.REGULAR((2,)),
         ],
         compiler_params=pltpu.CompilerParams(
             collective_id=0, has_side_effects=True, vmem_limit_bytes=56 * 1024 * 1024

time: 22.8 us -> 22.6 us (level)
  no operation moved by 1% of the time
where the time goes in v4:
time: 22.6 us; the launch traced here: 22.4 us
  Pallas kernels  21.8 us (96%)
  between operations  0.64 us (3%)
    pallas_call x1, Pallas kernels, on_device(): pl.pallas_call(functools.partial(kernel, T, L, E), out_shape=(buf(levels,...  20.8 us
    pallas_call x1, Pallas kernels, on_device(): pl.pallas_call(finish, out_shape=(jax.ShapeDtypeStruct((levels, crow, lon...  0.95 us

profile of v4, /device:TPU:0, one launch (start us, length us, event | category | flops | bytes accessed | tf_op | source)
XLA Modules:
  0.0 22.4 jit_solution(10411068916794806164)
XLA Ops:
  0.6 20.8 %shard_map.113 = (f32[4,16,1440]{2,1,0:T(8,128)S(1)}, f32[2,16,2,8,1440]{4,3,2,1,0:T(8,128)S(1)}, f32[32,1,128]{2,1,0:T(1,128)S(1)}) custom-call(s32[1,32]{1,0:T(1,128)} %rows_hbm.1, s32[1,32]{1,0:T(1,128)} %cnt_hbm.1, f32[16,32]{1,0:T(8,128)} %bitcast.18, f32[16,32]{1,0:T(8,128)} %bitcast.19, f32[4]{0:T(128)} %mp_hbm.1, f32[4,16,1440]{2,1,0:T(8,128)} %bitcast.15, ...), custom_call_target="tpu_custom_call" | custom-call | tf_op jit(solution)/shard_map/pallas_call | solution.py:654
  21.5 0.9 %shard_map.114 = (f32[4,16,1440]{2,1,0:T(8,128)}, f32[16,1440]{1,0:T(8,128)}) custom-call(f32[4,16,1440]{2,1,0:T(8,128)S(1)} %get-tuple-element.7.grad_v, f32[2,16,2,8,1440]{4,3,2,1,0:T(8,128)S(1)} %get-tuple-element.8.pert_v, f32[32,1,128]{2,1,0:T(1,128)S(1)} %get-tuple-element.9.cb_v), custom_call_target="tpu_custom_call" | custom-call | tf_op jit(solution)/shard_map/pallas_call | solution.py:686

commit v5 on v4

--- a/solution.py
+++ b/solution.py
@@ -47,7 +47,7 @@
     wide, coef, adj, h_first, h_last, h_after, h_before, a_up_v, a_down_v, a_after, a_before,
     end_v, lines, last, rims, nxt_v, prior_v, forc, edge, rs_v, edge_v, ca_send, ca_v, cb_send,
     load_sem, small_sem, h_ssem, h_rsem, a_ssem, a_rsem, t_ssem, t_rsem, e_ssem, e_rsem, p_ssem, p_rsem,
-    rs_ssem, rs_rsem, ed_ssem, ed_rsem, ca_ssem, ca_rsem, cb_ssem, cb_rsem, g_rsem, all_sem, round_sem,
+    rs_ssem, rs_rsem, ed_ssem, ed_rsem, sum_sem, g_rsem, round_sem,
 ):
     k, b, e = lax.axis_index("tm"), lax.axis_index("lat"), lax.axis_index("ens")
     _, half, crow, lon = fields.shape
@@ -72,6 +72,8 @@
 
     order = [lax.rem(shift(k, e) + t, half) for t in range(half)]
     level = [role * half + at for at in order]
+
+    ca_ssem, ca_rsem = sum_sem.at[0], sum_sem.at[1]
 
     def local(src, dst, sem):
         return pltpu.make_async_copy(src, dst, sem)
@@ -167,7 +169,7 @@
         pl.semaphore_wait(barrier, len(group) + L - 1)
         if direct:
             for db in range(1, L):
-                pl.semaphore_signal(all_sem, inc=1, device_id={"lat": lax.rem(b + db, L)}, device_id_type=MESH)
+                pl.semaphore_signal(round_sem.at[0], inc=1, device_id={"lat": lax.rem(b + db, L)}, device_id_type=MESH)
 
     h_up = [remote(h_last.at[t], h_before.at[t], h_ssem.at[0], h_rsem.at[0, t], up) for t in range(half)]
     h_down = [remote(h_first.at[t], h_after.at[t], h_ssem.at[1], h_rsem.at[1, t], down) for t in range(half)]
@@ -269,8 +271,8 @@
 
     def observe():
         def measure(base, carry):
-            for u in range(8):
-                j = base * 8 + u
+            for u in range(16):
+                j = base * 16 + u
                 row = rows_s[0, j]
                 slot = lax.rem(row // crow + half - shift(k, e), half)
                 row = lax.rem(row, crow)
@@ -280,7 +282,7 @@
                 part_v[j] = total
             return carry
 
-        lax.fori_loop(0, blocks // 8, measure, 0)
+        lax.fori_loop(0, blocks // 16, measure, 0)
         evolved = jnp.sum(part_v[...], axis=-1, keepdims=True)
         wgt[...] = prc_b[...] * (evolved - val_b[...])
         for c in range(0, tiles, 2):
@@ -530,7 +532,7 @@
     if direct:
         crowd = [(dt, lat, de) for lat in range(L) for dt in range(T) for de in range(E)]
         if not near:
-            pl.semaphore_wait(all_sem, L - 1)
+            pl.semaphore_wait(round_sem.at[0], L - 1)
     else:
         crowd = [(dt, b, de) for dt, de in group]
 
@@ -578,6 +580,7 @@
         part = ca_v[0]
         for at in range(1, T * E):
             part = part + ca_v[at]
+        cb_ssem, cb_rsem = sum_sem.at[2], sum_sem.at[3]
         cb_send[...] = part
         cb_v[b] = part
         for db in range(1, L):
@@ -671,7 +674,7 @@
             buf(half * E, 8, width), buf(2, half, 3, 1, width), buf(T, 8, width), buf(T, 3, 1, width),
             buf(1, 128), buf(T * E, 1, 128), buf(1, 128),
             dma((2,)), dma((4,)), dma((2,)), dma((2, half)), dma((2,)), dma((2,)), dma, dma((half,)), dma, dma,
-            dma, dma, dma, dma, dma((2,)), dma, dma, dma, dma, dma, dma, pltpu.SemaphoreType.REGULAR,
+            dma, dma, dma, dma, dma((2,)), dma, dma((2 if T * L * E <= 64 else 4,)), dma,
             pltpu.SemaphoreType.REGULAR((2,)),
         ],
         compiler_params=pltpu.CompilerParams(

time: 22.6 us -> 22.5 us (level)
  no operation moved by 1% of the time
where the time goes in v5:
time: 22.5 us; the launch traced here: 22.4 us
  Pallas kernels  21.7 us (96%)
  between operations  0.64 us (3%)
    pallas_call x1, Pallas kernels, on_device(): pl.pallas_call(functools.partial(kernel, T, L, E), out_shape=(buf(levels,...  20.8 us
    pallas_call x1, Pallas kernels, on_device(): pl.pallas_call(finish, out_shape=(jax.ShapeDtypeStruct((levels, crow, lon...  0.95 us

profile of v5, /device:TPU:0, one launch (start us, length us, event | category | flops | bytes accessed | tf_op | source)
XLA Modules:
  0.0 22.4 jit_solution(5584356988563468418)
XLA Ops:
  0.6 20.8 %shard_map.113 = (f32[4,16,1440]{2,1,0:T(8,128)S(1)}, f32[2,16,2,8,1440]{4,3,2,1,0:T(8,128)S(1)}, f32[32,1,128]{2,1,0:T(1,128)S(1)}) custom-call(s32[1,32]{1,0:T(1,128)} %rows_hbm.1, s32[1,32]{1,0:T(1,128)} %cnt_hbm.1, f32[16,32]{1,0:T(8,128)} %bitcast.18, f32[16,32]{1,0:T(8,128)} %bitcast.19, f32[4]{0:T(128)} %mp_hbm.1, f32[4,16,1440]{2,1,0:T(8,128)} %bitcast.15, ...), custom_call_target="tpu_custom_call" | custom-call | tf_op jit(solution)/shard_map/pallas_call | solution.py:657
  21.4 0.9 %shard_map.114 = (f32[4,16,1440]{2,1,0:T(8,128)}, f32[16,1440]{1,0:T(8,128)}) custom-call(f32[4,16,1440]{2,1,0:T(8,128)S(1)} %get-tuple-element.7.grad_v, f32[2,16,2,8,1440]{4,3,2,1,0:T(8,128)S(1)} %get-tuple-element.8.pert_v, f32[32,1,128]{2,1,0:T(1,128)S(1)} %get-tuple-element.9.cb_v), custom_call_target="tpu_custom_call" | custom-call | tf_op jit(solution)/shard_map/pallas_call | solution.py:689
